TPU v7x, 32 devices: a 4x4x1 block of a 4x4x8 slice. The times are simulated.
32 devices in a mesh: rep: 1 (over z), tp: 4 (over y), sp: 8 (over x, core).
Axes of the slice: x: 4, y: 4, z: 1, core: 2. Of those that a mesh axis runs over, the one named last changes fastest.
The devices are a block of a 4x4x8 slice.
Arguments:
- x_in: bfloat16 [4096, 5120], P(('rep', 'sp'))
- positions: int32 [4096], P(('rep', 'sp'))
- segments: int32 [4096], P(('rep', 'sp'))
- gain_attn: float32 [5120], replicated
- w_q: bfloat16 [5120, 4096], P(None, 'tp')
- w_k: bfloat16 [5120, 1024], P(None, 'tp')
- w_v: bfloat16 [5120, 1024], P(None, 'tp')
- w_o: bfloat16 [4096, 5120], P('tp')
- gain_mlp: float32 [5120], replicated
- w_gate: bfloat16 [5120, 32768], P(None, 'tp')
- w_up: bfloat16 [5120, 32768], P(None, 'tp')
- w_down: bfloat16 [32768, 5120], P('tp')
Outputs:
- output 1: bfloat16 [4096, 5120], P(('rep', 'sp'))
- output 2: bfloat16 [4096, 32, 128], P('rep', ('tp', 'sp'))
- output 3: bfloat16 [4096, 32, 128], P('rep', ('tp', 'sp'))
All inputs are finite; a program needn't handle non-finite values.
Results may differ from a plain program's by a relative error of at most 0.00708525.
Values are sent between devices in bfloat16 or wider.
A program may use at most 768 MiB of HBM per device.

v0:
```python
import jax
import jax.numpy as jnp
from jax import lax
from jax.sharding import PartitionSpec as P

HEAD_DIM = 128
ROPE_BASE = 500000.0
NORM_EPS = 1e-5
QUERY_ROWS = 512


def rms_norm(x_f32, gain_vec):
    mean_sq = jnp.mean(x_f32 * x_f32, axis=-1, keepdims=True)
    return (x_f32 * lax.rsqrt(mean_sq + NORM_EPS) * gain_vec).astype(jnp.bfloat16)


def rope_tables(positions):
    half_dim = HEAD_DIM // 2
    inv_freq = jnp.power(jnp.float32(ROPE_BASE), -jnp.arange(half_dim, dtype=jnp.float32) * (2.0 / HEAD_DIM))
    angles = positions.astype(jnp.float32)[..., None] * inv_freq
    return jnp.cos(angles)[..., None, :], jnp.sin(angles)[..., None, :]


def rotate(t_f32, cos_t, sin_t):
    half_dim = HEAD_DIM // 2
    t_lo = t_f32[..., :half_dim]
    t_hi = t_f32[..., half_dim:]
    return jnp.concatenate([t_lo * cos_t - t_hi * sin_t, t_hi * cos_t + t_lo * sin_t], axis=-1)


def project_qkv(x_f32, positions, gain_attn, w_q, w_k, w_v):
    row_count = x_f32.shape[0]
    u_norm = rms_norm(x_f32, gain_attn)
    cos_t, sin_t = rope_tables(positions)
    q_rot = rotate(jnp.dot(u_norm, w_q, preferred_element_type=jnp.float32).reshape(row_count, -1, HEAD_DIM), cos_t, sin_t).astype(jnp.bfloat16)
    k_rot = rotate(jnp.dot(u_norm, w_k, preferred_element_type=jnp.float32).reshape(row_count, -1, HEAD_DIM), cos_t, sin_t).astype(jnp.bfloat16)
    v_proj = jnp.dot(u_norm, w_v, preferred_element_type=jnp.float32).astype(jnp.bfloat16).reshape(row_count, -1, HEAD_DIM)
    return q_rot, k_rot, v_proj


def masked_attention(q_blk, key_rows, val_rows, q_index, k_index, q_seg, k_seg):
    scores = jnp.einsum("qhgc,shc->hgqs", q_blk, key_rows, preferred_element_type=jnp.float32) * (HEAD_DIM ** -0.5)
    allowed = (q_index[:, None] >= k_index[None, :]) & (q_seg[:, None] == k_seg[None, :])
    scores = jnp.where(allowed, scores, -1e30)
    row_max = jnp.max(scores, axis=-1, keepdims=True)
    weights = jnp.exp(scores - row_max)
    prob_bf16 = (weights / jnp.sum(weights, axis=-1, keepdims=True)).astype(jnp.bfloat16)
    return jnp.einsum("hgqs,shc->qhgc", prob_bf16, val_rows, preferred_element_type=jnp.float32).astype(jnp.bfloat16)


def mlp_tail(x_mid, gain_mlp, w_gate, w_up, w_down):
    u_mlp = rms_norm(x_mid, gain_mlp)
    gate_act = jnp.dot(u_mlp, w_gate, preferred_element_type=jnp.float32)
    up_act = jnp.dot(u_mlp, w_up, preferred_element_type=jnp.float32)
    hidden = (jax.nn.silu(gate_act) * up_act).astype(jnp.bfloat16)
    return (x_mid + lax.psum(jnp.dot(hidden, w_down, preferred_element_type=jnp.float32), "tp")).astype(jnp.bfloat16)


def solution(mesh):
    sp_size = mesh.shape["sp"]
    row_spec = P(("rep", "sp"), None)
    tok_spec = P(("rep", "sp"))
    full_spec = P(None)
    col_spec = P(None, "tp")
    wrow_spec = P("tp", None)
    cache_spec = P("rep", ("tp", "sp"), None)

    def local_layer(x_in, positions, segments, gain_attn, w_q, w_k, w_v, w_o, gain_mlp, w_gate, w_up, w_down):
        rows_local = x_in.shape[0]
        tokens = rows_local * sp_size
        heads_local = w_q.shape[1] // HEAD_DIM
        kv_local = w_k.shape[1] // HEAD_DIM
        kv_repeat = max(1, sp_size // kv_local)
        heads_dev = heads_local // sp_size
        slots_dev = kv_local * kv_repeat // sp_size
        group_size = heads_dev // slots_dev
        x_f32 = x_in.astype(jnp.float32)
        q_rot, k_rot, v_proj = project_qkv(x_f32, positions, gain_attn, w_q, w_k, w_v)
        k_send = jnp.repeat(k_rot, kv_repeat, axis=1).reshape(rows_local, sp_size, slots_dev, HEAD_DIM)
        v_send = jnp.repeat(v_proj, kv_repeat, axis=1).reshape(rows_local, sp_size, slots_dev, HEAD_DIM)
        send_buf = jnp.concatenate([q_rot.reshape(rows_local, sp_size, heads_dev, HEAD_DIM), k_send, v_send], axis=2)
        recv_buf = lax.all_to_all(send_buf, "sp", 1, 0, tiled=True).reshape(tokens, heads_dev + 2 * slots_dev, HEAD_DIM)
        seg_all = lax.all_gather(segments, "sp", tiled=True)
        q_all = recv_buf[:, :heads_dev].reshape(tokens, slots_dev, group_size, HEAD_DIM)
        k_all = recv_buf[:, heads_dev:heads_dev + slots_dev]
        v_all = recv_buf[:, heads_dev + slots_dev:]
        tok_index = jnp.arange(tokens)
        block_rows = min(tokens, QUERY_ROWS)
        pieces = []
        for block_idx in range(tokens // block_rows):
            row_start = block_idx * block_rows
            row_stop = row_start + block_rows
            pieces.append(masked_attention(q_all[row_start:row_stop], k_all[:row_stop], v_all[:row_stop],
                                           tok_index[row_start:row_stop], tok_index[:row_stop],
                                           seg_all[row_start:row_stop], seg_all[:row_stop]))
        attn_heads = jnp.concatenate(pieces, axis=0).reshape(sp_size, rows_local, heads_dev, HEAD_DIM)
        attn_local = lax.all_to_all(attn_heads, "sp", 0, 2, tiled=True).reshape(rows_local, heads_local * HEAD_DIM)
        x_mid = x_f32 + lax.psum(jnp.dot(attn_local, w_o, preferred_element_type=jnp.float32), "tp")
        y_out = mlp_tail(x_mid, gain_mlp, w_gate, w_up, w_down)
        return y_out, k_all, v_all

    return jax.shard_map(local_layer, mesh=mesh,
                         in_specs=(row_spec, tok_spec, tok_spec, full_spec, col_spec, col_spec, col_spec, wrow_spec,
                                   full_spec, col_spec, col_spec, wrow_spec),
                         out_specs=(row_spec, cache_spec, cache_spec), check_vma=False)
```

profile of v0, /device:TPU:97, one launch (start us, length us, event | category | flops | bytes accessed | tf_op | source)
XLA Modules:
  0.0 730.3 jit_solution(12529898453793514042)
XLA Ops:
  7.2 0.8 convert_element_type.128
  8.1 3.6 fusion
  11.7 0.5 multiply_cosine_fusion
  12.5 5.1 convolution_convert_fusion
  17.6 1.1 copy.49
  18.7 5.2 fusion.96
  24.2 10.0 %convolution_bitcast_fusion = f32[64,8,8,128]{3,1,2,0:T(8,128)S(1)} fusion(bf16[5120,1024]{1,0:T(8,128)(2,1)} %param.16, bf16[512,5120]{1,0:T(8,128)(2,1)} %param.12, f32[5120]{0:T(1024)S(1)} %copy-done.8, f32[512]{0:T(512)S(1)} %add_rsqrt_fusion.1), kind=kOutput, calls=%fused_computation.57 | convolution fusion | flops 5379194880 | bytes 17848320 | tf_op jit(solution)/shard_map/dot_general | solution.py:35
  34.2 0.5 copy.54
  34.7 0.7 fusion.100
  35.4 0.8 fusion.86
  36.5 2.0 pad_maximum_fusion
  38.5 6.3 all-to-all-start
  44.9 47.9 %all-gather = s32[8,1,512]{2,1,0:T(1,128)S(1)} all-gather(s32[1,1,512]{2,1,0:T(1,128)S(1)} %bitcast.339), channel_id=1, replica_groups=mesh['rep'=1,'tp'=4,'sp'=8] {'sp'}, dimensions={0}, use_global_device_ids=true | all-gather | bytes 18432 | tf_op jit(solution)/shard_map/all_gather | solution.py:83
  93.1 2.2 copy.50
  95.5 0.4 fusion.102
  96.1 0.3 fusion.47
  96.4 0.6 fusion.103
  97.1 0.4 fusion.23
  97.4 0.5 fusion.55
  98.0 0.8 fusion.104
  98.8 0.5 fusion.18
  99.3 0.7 fusion.83
  100.1 1.1 fusion.105
  101.1 0.6 fusion.12
  101.8 0.9 fusion.51
  102.7 1.3 fusion.106
  104.0 0.8 fusion.9
  104.8 1.1 fusion.77
  105.9 1.5 fusion.107
  107.5 1.3 fusion.8
  108.8 1.3 fusion.71
  110.1 1.8 fusion.108
  111.8 1.0 fusion.7
  112.9 1.5 fusion.65
  114.4 2.0 fusion.109
  116.4 1.2 fusion.6
  117.6 1.7 fusion.59
  119.3 0.4 copy.55
  120.0 23.2 %all_to_all.30 = bf16[8,512,1,128]{1,3,2,0:T(8,128)(2,1)S(1)} all-to-all(bf16[8,512,1,128]{1,3,2,0:T(8,128)(2,1)S(1)} %copy.51), channel_id=1, replica_groups=mesh['rep'=1,'tp'=4,'sp'=8] {'sp'}, dimensions={0} | all-to-all | bytes 2097152 | tf_op jit(solution)/shard_map/all_to_all | solution.py:97
  143.3 8.2 %fusion.110 = f32[512,5120]{1,0:T(8,128)} fusion(bf16[512,1024]{0,1:T(8,128)(2,1)S(1)} %bitcast.331, bf16[1024,5120]{1,0:T(8,128)(2,1)S(1)} %bitcast.311), kind=kOutput, calls=%fused_computation.158 | convolution fusion | flops 5368709120 | bytes 22020096 | tf_op jit(solution)/shard_map/dot_general | solution.py:98
  151.6 189.8 %all-reduce.3.cloned.1.call-done = f32[512,5120]{1,0:T(8,128)} async-done(((f32[512,5120]{1,0:T(8,128)}), f32[512,5120]{1,0:T(8,128)}) %all-reduce.3.cloned.1.call-update) | async-done | bytes 10485776 | tf_op jit(solution)/shard_map/psum | solution.py:98
  341.4 6.9 multiply_reduce_fusion
  348.3 10.2 %multiply_convert_fusion.1 = bf16[512,5120]{1,0:T(8,128)(2,1)} fusion(f32[5120]{0:T(1024)S(1)} %copy-done.6, f32[512]{0:T(512)S(1)} %add_rsqrt_fusion, f32[512,5120]{1,0:T(8,128)} %all-reduce.3.cloned.1.call-done, bf16[512,5120]{1,0:T(8,128)(2,1)} %param.12), kind=kLoop, calls=%fused_computation.8 | loop fusion | flops 13107200 | bytes 20994048 | tf_op jit(solution)/shard_map/convert_element_type | solution.py:14
  358.5 51.6 %fusion.111 = f32[512,8192]{1,0:T(8,128)} fusion(bf16[512,5120]{1,0:T(8,128)(2,1)} %multiply_convert_fusion.1, bf16[5120,8192]{1,0:T(8,128)(2,1)} %param.21), kind=kOutput, calls=%fused_computation.159 | convolution fusion | flops 42949672960 | bytes 105906176 | tf_op jit(solution)/shard_map/dot_general | solution.py:53
  410.1 58.0 %multiply_convert_fusion.clone.4 = bf16[512,8192]{1,0:T(8,128)(2,1)} fusion(f32[512,8192]{1,0:T(8,128)} %fusion.111, bf16[512,5120]{1,0:T(8,128)(2,1)} %multiply_convert_fusion.1, bf16[5120,8192]{1,0:T(8,128)(2,1)} %param.22), kind=kOutput, calls=%fused_computation.clone.clone.clone.1 | convolution fusion | flops 42974838784 | bytes 114294784 | tf_op jit(solution)/shard_map/dot_general | solution.py:54
  468.1 54.2 %fusion.3 = f32[512,5120]{1,0:T(8,128)} fusion(bf16[8192,5120]{1,0:T(8,128)(2,1)} %param.23, bf16[512,8192]{1,0:T(8,128)(2,1)} %multiply_convert_fusion.clone.4), kind=kOutput, calls=%fused_computation.10 | convolution fusion | flops 42949672960 | bytes 102760448 | tf_op jit(solution)/shard_map/dot_general | solution.py:56
  522.3 188.8 %all-reduce.5.cloned.1.call-done = f32[512,5120]{1,0:T(8,128)} async-done(((f32[512,5120]{1,0:T(8,128)}), f32[512,5120]{1,0:T(8,128)}) %all-reduce.5.cloned.1.call-update) | async-done | bytes 10485776 | tf_op jit(solution)/shard_map/psum | solution.py:56
  711.1 11.9 %add_convert_fusion = bf16[512,5120]{1,0:T(8,128)(2,1)} fusion(f32[512,5120]{1,0:T(8,128)} %all-reduce.5.cloned.1.call-done, f32[512,5120]{1,0:T(8,128)} %all-reduce.3.cloned.1.call-done, bf16[512,5120]{1,0:T(8,128)(2,1)} %param.12), kind=kLoop, calls=%fused_computation.7 | loop fusion | flops 10485760 | bytes 31457280 | tf_op jit(solution)/shard_map/convert_element_type | solution.py:56
  (70 shorter events, 1.9 us)
Async XLA Ops:
  7.2 5.3 copy-start
  7.2 5.3 copy-start.8
  36.5 8.4 %copy-start.7 = (s32[512]{0:T(512)S(1)}, s32[512]{0:T(512)}, u32[]{:S(2)}) copy-start(s32[512]{0:T(512)} %param.14) | copy-start | bytes 6148
  38.5 54.6 %all-to-all-start = ((bf16[512,8,3,128]{3,0,2,1:T(8,128)(2,1)}), bf16[512,8,3,128]{3,0,2,1:T(8,128)(2,1)}, u32[]{:S(2)}, u32[]{:S(2)}) async-start(bf16[512,8,3,128]{3,0,2,1:T(8,128)(2,1)} %pad_maximum_fusion), calls=%async_computation | async-start | bytes 6291456 | tf_op jit(solution)/shard_map/all_to_all | solution.py:82
  44.9 296.5 %all-reduce.3.cloned.1.call-start = ((), (), s32[]{:S(2)}) async-start(), calls=%async_computation.2 | async-start | bytes 20971520 | tf_op jit(solution)/shard_map/psum | solution.py:98
  92.8 2.7 copy-start.4
  95.5 18.9 %copy-start.3 = (bf16[4096,1,128]{2,0,1:T(8,128)(2,1)}, bf16[4096,1,128]{2,0,1:T(8,128)(2,1)S(1)}, u32[]{:S(2)}) copy-start(bf16[4096,1,128]{2,0,1:T(8,128)(2,1)S(1)} %get-tuple-element.6) | copy-start | bytes 3145732
  95.5 22.1 %copy-start.2 = (bf16[4096,1,128]{2,0,1:T(8,128)(2,1)}, bf16[4096,1,128]{2,0,1:T(8,128)(2,1)S(1)}, u32[]{:S(2)}) copy-start(bf16[4096,1,128]{2,0,1:T(8,128)(2,1)S(1)} %get-tuple-element.5) | copy-start | bytes 3145732
  95.5 1.0 slice-start.3
  99.3 0.7 slice-start.4
  104.8 1.1 slice-start.5
  112.9 1.5 copy-start.5
  117.6 25.7 %slice-start = ((s8[10485760]{0:T(1024)(128)(4,1)}), s8[4194304]{0:T(1024)(128)(4,1)S(1)}, s32[]{:S(2)}) async-start(s8[10485760]{0:T(1024)(128)(4,1)} %bitcast.310), calls=%async_computation.4 | async-start | bytes 8388608
  117.6 25.6 %slice-start.1 = ((s8[10485760]{0:T(1024)(128)(4,1)}), s8[4194304]{0:T(1024)(128)(4,1)S(1)}, s32[]{:S(2)}) async-start(s8[10485760]{0:T(1024)(128)(4,1)} %bitcast.310), calls=%async_computation.5 | async-start | bytes 8388608
  117.6 25.6 %slice-start.2 = ((s8[10485760]{0:T(1024)(128)(4,1)}), s8[2097152]{0:T(1024)(128)(4,1)S(1)}, s32[]{:S(2)}) async-start(s8[10485760]{0:T(1024)(128)(4,1)} %bitcast.310), calls=%async_computation.6 | async-start | bytes 4194304
  151.6 196.8 %copy-start.6 = (f32[5120]{0:T(1024)S(1)}, f32[5120]{0:T(1024)}, u32[]{:S(2)}) copy-start(f32[5120]{0:T(1024)} %param.20) | copy-start | bytes 61444
  151.6 559.6 %all-reduce.5.cloned.1.call-start = ((), (), s32[]{:S(2)}) async-start(), calls=%async_computation.3 | async-start | bytes 20971520 | tf_op jit(solution)/shard_map/psum | solution.py:56
  711.1 11.9 %copy-start.1 = (bf16[5120,256]{1,0:T(8,128)(2,1)S(1)}, bf16[5120,256]{1,0:T(8,128)(2,1)}, u32[]{:S(2)}) copy-start(bf16[5120,256]{1,0:T(8,128)(2,1)} %param.18) | copy-start | bytes 7864324
Sparse Core Ops, SparseCore 0:
  151.7 189.6 all-reduce.2
  522.4 188.6 all-reduce.4
where the time goes:
time: 739 us; the launch traced here: 730 us
  waiting for transfers between devices  379 us (51%)
  matrix products  210 us (28%)
  blocking collectives  71.1 us (10%)
  other arithmetic  42.9 us (6%)
  between operations  15 us (2%)
    psum x1, waiting for transfers between devices, local_layer(): lax.psum(jnp.dot(attn_local, w_o, preferred_element_type=jnp.float32), 'tp')  190 us
    psum x1, waiting for transfers between devices, mlp_tail(): lax.psum(jnp.dot(hidden, w_down, preferred_element_type=jnp.float32), 'tp')  189 us
    dot_general x1, matrix products, mlp_tail(): up_act = jnp.dot(u_mlp, w_up, preferred_element_type=jnp.float32)  58 us
    dot_general x1, matrix products, mlp_tail(): jnp.dot(hidden, w_down, preferred_element_type=jnp.float32)  54.2 us
    dot_general x1, matrix products, mlp_tail(): gate_act = jnp.dot(u_mlp, w_gate, preferred_element_type=jnp.float32)  51.6 us
    all_gather x1, blocking collectives, local_layer(): seg_all = lax.all_gather(segments, 'sp', tiled=True)  47.9 us
    all_to_all x1, blocking collectives, local_layer(): lax.all_to_all(attn_heads, 'sp', 0, 2, tiled=True)  23.2 us
  transfers between devices with their start and end apart: 3, of which 2 were waited for; matrix products, arithmetic and copies ran while one was open for 0% of the time, Pallas kernels for 0%

commit v1 on v0

--- a/solution.py
+++ b/solution.py
@@ -1,6 +1,10 @@
+import functools
+
 import jax
 import jax.numpy as jnp
 from jax import lax
+from jax.experimental import pallas as pl
+from jax.experimental.pallas import tpu as pltpu
 from jax.sharding import PartitionSpec as P
 
 HEAD_DIM = 128
@@ -48,12 +52,400 @@
     return jnp.einsum("hgqs,shc->qhgc", prob_bf16, val_rows, preferred_element_type=jnp.float32).astype(jnp.bfloat16)
 
 
-def mlp_tail(x_mid, gain_mlp, w_gate, w_up, w_down):
-    u_mlp = rms_norm(x_mid, gain_mlp)
-    gate_act = jnp.dot(u_mlp, w_gate, preferred_element_type=jnp.float32)
-    up_act = jnp.dot(u_mlp, w_up, preferred_element_type=jnp.float32)
-    hidden = (jax.nn.silu(gate_act) * up_act).astype(jnp.bfloat16)
-    return (x_mid + lax.psum(jnp.dot(hidden, w_down, preferred_element_type=jnp.float32), "tp")).astype(jnp.bfloat16)
+MESH = pl.DeviceIdType.MESH
+BF16, F32 = jnp.bfloat16, jnp.float32
+VMEM_BYTES = 63 * 2 ** 20
+
+
+def mlp_kernel(chunks, cb, attn, wo, x_hbm, gain, wg, wu, wd, y_hbm,
+               wbuf, hbuf, xmid, srow, sin, p_own, p_out, d_in, f_in, e_in, ystage, *rest):
+    n_ch = len(chunks)
+    u2 = rest[:n_ch]
+    (wsem, asem, xsem, s_s, s_r, u1s, u1r, u2s, u2r, ups, upr,
+     d_s, d_r, f_s, f_r, e_s, e_r, a_l, a_s, a_r, h_s, h_r) = rest[n_ch:]
+    rows, dim = x_hbm.shape
+    depth = attn.shape[1]
+    tp = lax.axis_size("tp")
+    col = dim // tp
+    nb = col // cb
+    ff = wg.shape[1] // 2
+    y = lax.axis_index("tp")
+    s = lax.axis_index("sp")
+    core = s % 2
+    pair = s + 1 - 2 * core
+    yp, ym, y2 = (y + 1) % tp, (y + tp - 1) % tp, (y + 2) % tp
+    here = {"tp": y, "sp": s}
+    to_pair, to_p, to_m, to_2 = ({"tp": y, "sp": pair}, {"tp": yp, "sp": s}, {"tp": ym, "sp": s}, {"tp": y2, "sp": s})
+    starts = [sum(chunks[:i]) for i in range(n_ch)]
+    n_g, n_d = ff // cb, tp * nb // 2
+
+    def remote(src, dst, ssem, rsem, to):
+        return pltpu.make_async_remote_copy(src, dst, ssem, rsem, device_id=to, device_id_type=MESH)
+
+    def cols(block, width=None):
+        return pl.ds(pl.multiple_of(block * (width or cb), 128), width or cb)
+
+    def w_o_tile(t, slot):
+        width = min(2 * cb, col - t * 2 * cb)
+        return [pltpu.make_async_copy(wo.at[:, pl.ds(t * 2 * cb, width)],
+                                      wbuf.at[slot, pl.ds(0, depth), pl.ds(0, width)], wsem.at[slot, 0])]
+
+    def g_tile(n, slot):
+        c = pl.ds(pl.multiple_of(core * ff + n * cb, 128), cb)
+        return [pltpu.make_async_copy(wg.at[:, c], wbuf.at[slot, :, pl.ds(0, cb)], wsem.at[slot, 0]),
+                pltpu.make_async_copy(wu.at[:, c], wbuf.at[slot, :, pl.ds(cb, cb)], wsem.at[slot, 1])]
+
+    def d_cols(m):
+        q = m // nb
+        d = (2 + 3 * q + 3 * (q * (q - 1) // 2)) % 4
+        return pl.ds(pl.multiple_of(((y + d) % tp) * col + (m % nb) * cb, 128), cb)
+
+    def d_tile(p, slot):
+        r = pl.ds(pl.multiple_of(core * ff, 128), ff)
+        return [pltpu.make_async_copy(wd.at[r, d_cols(2 * p + i)], wbuf.at[slot, pl.ds(0, ff), pl.ds(i * cb, cb)],
+                                      wsem.at[slot, i]) for i in range(2)]
+
+    def start(copies):
+        for c in copies:
+            c.start()
+
+    def wait(copies):
+        for c in copies:
+            c.wait()
+
+    n_o = -(-col // (2 * cb))
+    a_copy = pltpu.make_async_copy(attn, hbuf.at[pl.ds(0, rows), pl.ds(0, depth)], asem)
+    a_copy.start()
+    x_copies = [pltpu.make_async_copy(x_hbm.at[pl.ds(r0, r), cols(y, col)], u2[i].at[pl.ds(0, r), cols(y, col)], xsem.at[i])
+                for i, (r0, r) in enumerate(zip(starts, chunks))]
+    start(w_o_tile(0, 0))
+    start(w_o_tile(1, 1))
+    start(x_copies)
+
+    barrier = pltpu.get_barrier_semaphore()
+    for to in (to_pair, to_p, to_m, to_2):
+        pl.semaphore_signal(barrier, inc=1, device_id=to, device_id_type=MESH)
+    pl.semaphore_wait(barrier, 4)
+
+    a_copy.wait()
+    wait(x_copies)
+    for t in range(n_o):
+        if t + 2 < n_o:
+            start(w_o_tile(t + 2, (t + 2) % 3))
+        else:
+            start(g_tile(t + 2 - n_o, (t + 2) % 3))
+        wait(w_o_tile(t, t % 3))
+        width = min(2 * cb, col - t * 2 * cb)
+        xmid[:, pl.ds(t * 2 * cb, width)] = jnp.dot(hbuf[pl.ds(0, rows), pl.ds(0, depth)],
+                                                    wbuf[t % 3, pl.ds(0, depth), pl.ds(0, width)],
+                                                    preferred_element_type=F32)
+    sq = jnp.zeros((rows, 128), F32)
+    for i, (r0, r) in enumerate(zip(starts, chunks)):
+        xmid[pl.ds(r0, r), :] += u2[i][pl.ds(0, r), cols(y, col)].astype(F32)
+    for b in range(col // 128):
+        v = xmid[:, pl.ds(b * 128, 128)]
+        sq += v * v
+    tot = jnp.broadcast_to(jnp.sum(sq, axis=1, keepdims=True), (rows, 128)).T
+    srow[...] = tot[:8, :]
+    stat = [remote(srow, sin.at[i], s_s.at[i], s_r.at[i], to) for i, to in enumerate((to_p, to_m, to_2))]
+    start(stat)
+    wait(stat)
+    tot = srow[...] + sin[0] + sin[1] + sin[2]
+    inv = lax.rsqrt(tot * (1.0 / dim) + NORM_EPS)
+    inv_col = jnp.broadcast_to(inv[:1, :], (128, rows)).T
+
+    def norm_chunk(i):
+        r0, r = starts[i], chunks[i]
+        for b in range(col // 128):
+            c = pl.ds(pl.multiple_of(y * col + b * 128, 128), 128)
+            u2[i][pl.ds(0, r), c] = (xmid[pl.ds(r0, r), pl.ds(b * 128, 128)] * inv_col[r0:r0 + r, :]
+                                     * gain[:, c]).astype(BF16)
+
+    def blk(i, row0, n_rows, rank):
+        return u2[i].at[pl.ds(row0, n_rows), cols(rank, col)]
+
+    def u_first(i):
+        r = chunks[i]
+        return [remote(blk(i, 0, r, y), blk(i, 0, r, y), u1s.at[i, 0], u1r.at[i, 1], to_p),
+                remote(blk(i, 0, r, y), blk(i, 0, r, y), u1s.at[i, 1], u1r.at[i, 0], to_m)]
+
+    def u_pair(i, j):
+        r, rank = chunks[i], (y, yp, ym, y2)[j]
+        return remote(blk(i, 0, r, rank), blk(i, r, r, rank), ups.at[i, j], upr.at[i, j], to_pair)
+
+    def u_second(i):
+        h = chunks[i] // 2
+        return [remote(blk(i, h, h, yp), blk(i, h, h, yp), u2s.at[i, 0], u2r.at[i, 0], to_m),
+                remote(blk(i, 0, h, ym), blk(i, 0, h, ym), u2s.at[i, 1], u2r.at[i, 1], to_p)]
+
+    def u_start(i):
+        start(u_first(i))
+        u_pair(i, 0).start()
+
+    def u_mid(i):
+        first, second = u_first(i), u_second(i)
+        first[1].wait_recv()
+        second[0].start()
+        u_pair(i, 1).start()
+        first[0].wait_recv()
+        second[1].start()
+        u_pair(i, 2).start()
+
+    def u_last(i):
+        for c in u_second(i):
+            c.wait_recv()
+        u_pair(i, 3).start()
+
+    def u_ready(i):
+        for j in range(4):
+            u_pair(i, j).wait_recv()
+
+    def u_drain(i):
+        for c in u_first(i) + u_second(i) + [u_pair(i, j) for j in range(4)]:
+            c.wait_send()
+
+    def bi(d, k):
+        return {2: 0, 1: 1, 3: 2, 0: 3}[d] * nb + k
+
+    def d_copy(i, m):
+        r, par = chunks[i], i % 2
+        return remote(p_out.at[m % 4, pl.ds(0, r)], d_in.at[par, m, pl.ds(0, r)], d_s.at[m % 4], d_r.at[par, m], to_pair)
+
+    def t_add(i, m):
+        r, par = chunks[i], i % 2
+        d_copy(i, m).wait_recv()
+        p_own[m, pl.ds(0, r)] += d_in[par, m, pl.ds(0, r)]
+
+    def f_copies(i, k):
+        h, par = chunks[i] // 2, i % 2
+        return [remote(p_own.at[k, pl.ds(0, h)], f_in.at[par, 0, k, pl.ds(0, h)], f_s.at[0, k], f_r.at[par, 0, k], to_m),
+                remote(p_own.at[k, pl.ds(h, h)], f_in.at[par, 1, k, pl.ds(0, h)], f_s.at[1, k], f_r.at[par, 1, k], to_p)]
+
+    def e_copies(i, k):
+        r, par = chunks[i], i % 2
+        return [remote(p_own.at[2 * nb + k, pl.ds(0, r)], e_in.at[par, 0, k, pl.ds(0, r)], e_s.at[0, k], e_r.at[par, 0, k], to_m),
+                remote(p_own.at[nb + k, pl.ds(0, r)], e_in.at[par, 1, k, pl.ds(0, r)], e_s.at[1, k], e_r.at[par, 1, k], to_p)]
+
+    def t_e(i, k, side):
+        h, par = chunks[i] // 2, i % 2
+        f_copies(i, k)[side].wait_recv()
+        m, r0 = (2 * nb + k, 0) if side == 0 else (nb + k, h)
+        p_own[m, pl.ds(r0, h)] += f_in[par, side, k, pl.ds(0, h)]
+        e_copies(i, k)[side].start()
+
+    def y_at(i, row0, n_rows, rank, k):
+        return y_hbm.at[pl.ds(starts[i] + row0, n_rows), pl.ds(pl.multiple_of(rank * col + k * cb, 128), cb)]
+
+    def a_copies(i, k):
+        r, par = chunks[i], i % 2
+        src = ystage.at[par, k, pl.ds(0, r)]
+        return [remote(src, y_at(i, 0, r, y, k), a_s.at[par, 0, k], a_r.at[par, 1, k], to_p),
+                remote(src, y_at(i, 0, r, y, k), a_s.at[par, 1, k], a_r.at[par, 0, k], to_m)]
+
+    def a_local(i, k):
+        r, par = chunks[i], i % 2
+        return pltpu.make_async_copy(ystage.at[par, k, pl.ds(0, r)], y_at(i, 0, r, y, k), a_l.at[par, k])
+
+    def h_copies(i, k):
+        h, par = chunks[i] // 2, i % 2
+        return [remote(y_at(i, h, h, yp, k), y_at(i, h, h, yp, k), h_s.at[par, 0, k], h_r.at[par, 0, k], to_m),
+                remote(y_at(i, 0, h, ym, k), y_at(i, 0, h, ym, k), h_s.at[par, 1, k], h_r.at[par, 1, k], to_p)]
+
+    def t_final(i, k):
+        r, par = chunks[i], i % 2
+        for c in e_copies(i, k):
+            c.wait_recv()
+        v = (p_own[3 * nb + k, pl.ds(0, r)] + e_in[par, 0, k, pl.ds(0, r)] + e_in[par, 1, k, pl.ds(0, r)]
+             + xmid[pl.ds(starts[i], r), cols(k)])
+        ystage[par, k, pl.ds(0, r)] = v.astype(BF16)
+        start(a_copies(i, k))
+        a_local(i, k).start()
+
+    def t_fwd(i, k):
+        first, second = a_copies(i, k), h_copies(i, k)
+        first[1].wait_recv()
+        second[0].start()
+        first[0].wait_recv()
+        second[1].start()
+
+    def t_halves(i, k):
+        for c in h_copies(i, k):
+            c.wait_recv()
+
+    def t_drain(i, k):
+        for c in f_copies(i, k) + e_copies(i, k) + a_copies(i, k) + h_copies(i, k):
+            c.wait_send()
+        a_local(i, k).wait()
+
+    norm_chunk(0)
+    u_start(0)
+    for i in range(1, n_ch):
+        norm_chunk(i)
+    u_mid(0)
+    if n_ch > 1:
+        u_start(1)
+    u_last(0)
+    u_ready(0)
+
+    base = n_o
+    for i in range(n_ch):
+        r = chunks[i]
+        g_base, d_base = base % 3, (base + n_g) % 3
+        base += n_g + n_d
+
+        @pl.loop(0, n_g)
+        def _(n, i=i, r=r, g_base=g_base):
+            nxt = (g_base + n + 2) % 3
+
+            @pl.when(n + 2 < n_g)
+            def _():
+                start(g_tile(n + 2, nxt))
+
+            @pl.when(n + 2 >= n_g)
+            def _():
+                start(d_tile(n + 2 - n_g, nxt))
+
+            slot = (g_base + n) % 3
+            wait(g_tile(n, slot))
+            g = jnp.dot(u2[i][...], wbuf[slot], preferred_element_type=F32)
+            hbuf[pl.ds(0, 2 * r), cols(n)] = (jax.nn.silu(g[:, :cb]) * g[:, cb:]).astype(BF16)
+
+            if i == 0:
+                for j in range(1, n_ch):
+                    t0 = G_U[0] + (j - 1) * G_U[2]
+
+                    @pl.when(n == t0)
+                    def _(j=j):
+                        u_mid(j)
+                        if j + 1 < n_ch:
+                            u_start(j + 1)
+
+                    @pl.when(n == t0 + G_U[1])
+                    def _(j=j):
+                        u_last(j)
+            else:
+                for k in range(nb):
+                    @pl.when(n == G_E[0] + G_E[1] * k)
+                    def _(k=k):
+                        t_final(i - 1, k)
+
+                    @pl.when(n == G_F[0] + G_F[1] * k)
+                    def _(k=k):
+                        t_fwd(i - 1, k)
+
+                @pl.when(n == n_g - 1)
+                def _():
+                    for k in range(nb):
+                        t_halves(i - 1, k)
+                    for k in range(nb):
+                        t_drain(i - 1, k)
+
+        @pl.loop(0, n_d)
+        def _(p, i=i, r=r, d_base=d_base):
+            nxt = (d_base + p + 2) % 3
+
+            @pl.when(p + 2 < n_d)
+            def _():
+                start(d_tile(p + 2, nxt))
+
+            if i + 1 < n_ch:
+                @pl.when(p + 2 >= n_d)
+                def _():
+                    start(g_tile(p + 2 - n_d, nxt))
+
+            slot = (d_base + p) % 3
+            wait(d_tile(p, slot))
+            v = jnp.dot(hbuf[pl.ds(0, 2 * r), :], wbuf[slot, pl.ds(0, ff)], preferred_element_type=F32)
+            for q in range(2):
+                m = 2 * p + q
+                p_own[m, pl.ds(0, r)] = v[:r, q * cb:(q + 1) * cb]
+
+                @pl.when(p >= 2)
+                def _(m=m):
+                    d_copy(i, m).wait_send()
+
+                p_out[m % 4, pl.ds(0, r)] = v[r:, q * cb:(q + 1) * cb]
+                d_copy(i, m).start()
+
+            @pl.when(p >= 1)
+            def _():
+                for q in range(2):
+                    t_add(i, 2 * p - 2 + q)
+
+            for k in range(nb):
+                @pl.when(p == (k // 2) + 1)
+                def _(k=k):
+                    start(f_copies(i, k))
+            for k in range(nb):
+                for side, at in ((1, D_E1[k]), (0, D_E0[k])):
+                    if at < n_d:
+                        @pl.when(p == at)
+                        def _(k=k, side=side):
+                            t_e(i, k, side)
+
+        for q in range(2):
+            t_add(i, 2 * n_d - 2 + q)
+        for k in range(nb):
+            for side, at in ((1, D_E1[k]), (0, D_E0[k])):
+                if at >= n_d:
+                    t_e(i, k, side)
+        for q in range(4):
+            d_copy(i, 2 * n_d - 4 + q).wait_send()
+        if i + 1 < n_ch:
+            u_ready(i + 1)
+
+    last = n_ch - 1
+    for k in range(nb):
+        t_final(last, k)
+        if k >= 2:
+            t_fwd(last, k - 2)
+    for k in range(nb - 2, nb):
+        t_fwd(last, k)
+    for k in range(nb):
+        t_halves(last, k)
+    for k in range(nb):
+        t_drain(last, k)
+    for i in range(n_ch):
+        u_drain(i)
+
+
+CHUNKS = (256, 256)
+G_U = (5, 4, 8)
+G_E = (2, 2)
+G_F = (6, 2)
+D_E1 = (4, 5, 6, 7, 8)
+D_E0 = (6, 7, 8, 9, 10)
+
+
+def mlp_call(attn, wo, x_in, gain, wg, wu, wd):
+    rows, dim = x_in.shape
+    tp = lax.axis_size("tp")
+    col, cb = dim // tp, 256
+    nb = col // cb
+    ff = wg.shape[1] // 2
+    chunks = CHUNKS
+    n_ch, rm = len(chunks), max(chunks)
+    hb = tp * nb
+    dma = pltpu.SemaphoreType.DMA
+    anyspec = pl.BlockSpec(memory_space=pl.ANY)
+    scratch = [
+        pltpu.VMEM((3, dim, 2 * cb), BF16), pltpu.VMEM((max(rows, 2 * rm), max(ff, attn.shape[1])), BF16),
+        pltpu.VMEM((rows, col), F32), pltpu.VMEM((8, rows), F32), pltpu.VMEM((tp - 1, 8, rows), F32),
+        pltpu.VMEM((hb, rm, cb), F32), pltpu.VMEM((4, rm, cb), F32), pltpu.VMEM((2, hb, rm, cb), F32),
+        pltpu.VMEM((2, 2, nb, rm // 2, cb), F32), pltpu.VMEM((2, 2, nb, rm, cb), F32), pltpu.VMEM((2, nb, rm, cb), BF16),
+        *[pltpu.VMEM((2 * r, dim), BF16) for r in chunks],
+        dma((3, 2)), dma(()), dma((n_ch,)), dma((3,)), dma((3,)),
+        dma((n_ch, 2)), dma((n_ch, 2)), dma((n_ch, 2)), dma((n_ch, 2)), dma((n_ch, 4)), dma((n_ch, 4)),
+        dma((4,)), dma((2, hb)), dma((2, nb)), dma((2, 2, nb)), dma((2, nb)), dma((2, 2, nb)),
+        dma((2, nb)), dma((2, 2, nb)), dma((2, 2, nb)), dma((2, 2, nb)), dma((2, 2, nb)),
+    ]
+    return pl.pallas_call(
+        functools.partial(mlp_kernel, chunks, cb), name="mlp",
+        out_shape=jax.ShapeDtypeStruct((rows, dim), BF16),
+        in_specs=[anyspec, anyspec, anyspec, pl.BlockSpec(memory_space=pltpu.VMEM), anyspec, anyspec, anyspec],
+        out_specs=anyspec, scratch_shapes=scratch,
+        compiler_params=pltpu.CompilerParams(collective_id=1, has_side_effects=True, vmem_limit_bytes=VMEM_BYTES),
+    )(attn, wo, x_in, gain.reshape(1, dim), wg, wu, wd)
 
 
 def solution(mesh):
@@ -95,8 +487,9 @@
                                            seg_all[row_start:row_stop], seg_all[:row_stop]))
         attn_heads = jnp.concatenate(pieces, axis=0).reshape(sp_size, rows_local, heads_dev, HEAD_DIM)
         attn_local = lax.all_to_all(attn_heads, "sp", 0, 2, tiled=True).reshape(rows_local, heads_local * HEAD_DIM)
-        x_mid = x_f32 + lax.psum(jnp.dot(attn_local, w_o, preferred_element_type=jnp.float32), "tp")
-        y_out = mlp_tail(x_mid, gain_mlp, w_gate, w_up, w_down)
+        attn_full = lax.all_gather(attn_local, "tp", axis=1, tiled=True)
+        wo_cols = lax.all_to_all(w_o, "tp", 1, 0, tiled=True)
+        y_out = mlp_call(attn_full, wo_cols, x_in, gain_mlp, w_gate, w_up, w_down)
         return y_out, k_all, v_all
 
     return jax.shard_map(local_layer, mesh=mesh,

time: 739 us -> 564 us (0.76)
  Pallas kernels: 0 us -> 246 us
  waiting for transfers between devices: 379 us -> 154 us
  matrix products: 210 us -> 38.1 us
  other arithmetic: 42.9 us -> 13.8 us
  blocking collectives: 71.1 us -> 47.7 us
  starting transfers between devices: 6.42 us -> 21.4 us
  local copies, waits for them, and re-layouts: 6.16 us -> 19.4 us
    psum x2 -> x0, waiting for transfers between devices: 379 us -> none  [the longest x1 190 us: local_layer(): lax.psum(jnp.dot(attn_local, w_o, preferred_element_type=jnp.float32), 'tp')]
    pallas_call x0 -> x1, Pallas kernels: none -> 246 us  [mlp_call(): pl.pallas_call(functools.partial(mlp_kernel, chunks, cb), name='mlp', out...]
    dot_general x4 -> x0, matrix products: 172 us -> none  [the longest x1 58 us: mlp_tail(): up_act = jnp.dot(u_mlp, w_up, preferred_element_type=jnp.float32)]
    all_to_all x0 -> x2, waiting for transfers between devices: none -> 154 us  [the longest x1 148 us: local_layer(): wo_cols = lax.all_to_all(w_o, 'tp', 1, 0, tiled=True)]
    all_to_all x1 -> x0, blocking collectives: 23.2 us -> none  [local_layer(): lax.all_to_all(attn_heads, 'sp', 0, 2, tiled=True)]
    convert_element_type x2 -> x0, other arithmetic: 22 us -> none  [the longest x1 11.9 us: mlp_tail(): (x_mid + lax.psum(jnp.dot(hidden, w_down, preferred_element_type=jnp.floa...]
    all_to_all x0 -> x2, starting transfers between devices: none -> 15.1 us  [the longest x1 9 us: local_layer(): lax.all_to_all(attn_heads, 'sp', 0, 2, tiled=True)]
    all_to_all x0 -> x2, local copies, waits for them, and re-layouts: none -> 9.17 us  [the longest x1 8.49 us: local_layer(): wo_cols = lax.all_to_all(w_o, 'tp', 1, 0, tiled=True)]
  transfers between devices with their start and end apart: 3 -> 4, of which waited for: 2 -> 2; matrix products, arithmetic and copies ran while one was open for 0% -> 2% of each run, Pallas kernels for 0% -> 0%
where the time goes in v1:
time: 564 us; the launch traced here: 555 us
  Pallas kernels  246 us (44%)
  waiting for transfers between devices  154 us (27%)
  blocking collectives  47.7 us (8%)
  matrix products  38.1 us (7%)
  starting transfers between devices  21.4 us (4%)
  local copies, waits for them, and re-layouts  19.4 us (3%)
  between operations  14.7 us (3%)
  other arithmetic  13.8 us (2%)
    pallas_call x1, Pallas kernels, mlp_call(): pl.pallas_call(functools.partial(mlp_kernel, chunks, cb), name='mlp', out...  246 us
    all_to_all x1, waiting for transfers between devices, local_layer(): wo_cols = lax.all_to_all(w_o, 'tp', 1, 0, tiled=True)  148 us
    all_gather x1, blocking collectives, local_layer(): seg_all = lax.all_gather(segments, 'sp', tiled=True)  47.7 us
  transfers between devices with their start and end apart: 4, of which 2 were waited for; matrix products, arithmetic and copies ran while one was open for 2% of the time, Pallas kernels for 0%

profile of v1, /device:TPU:97, one launch (start us, length us, event | category | flops | bytes accessed | tf_op | source)
XLA Modules:
  0.0 555.0 jit_solution(9958892739464068419)
XLA Ops:
  7.2 0.7 convert_element_type.119
  7.9 3.6 fusion
  11.5 0.5 multiply_cosine_fusion
  12.3 5.2 convolution_convert_fusion
  17.7 5.2 fusion.93
  23.2 10.0 %convolution_bitcast_fusion = f32[64,8,8,128]{3,1,2,0:T(8,128)S(1)} fusion(bf16[5120,1024]{1,0:T(8,128)(2,1)} %param.16, bf16[512,5120]{1,0:T(8,128)(2,1)} %x_hbm.1, f32[5120]{0:T(1024)S(1)} %copy-done.5, f32[512]{0:T(512)S(1)} %add_rsqrt_fusion), kind=kOutput, calls=%fused_computation.51 | convolution fusion | flops 5379194880 | bytes 17848320 | tf_op jit(solution)/shard_map/dot_general | solution.py:39
  33.2 0.5 copy.58
  33.7 0.7 fusion.97
  34.4 0.8 fusion.84
  35.5 2.0 pad_maximum_fusion
  37.5 6.1 %all-to-all-start = ((bf16[512,8,3,128]{3,0,2,1:T(8,128)(2,1)}), bf16[512,8,3,128]{3,0,2,1:T(8,128)(2,1)S(1)}, u32[]{:S(2)}, u32[]{:S(2)}) async-start(bf16[512,8,3,128]{3,0,2,1:T(8,128)(2,1)} %pad_maximum_fusion), calls=%async_computation | async-start | bytes 6291456 | tf_op jit(solution)/shard_map/all_to_all | solution.py:474
  43.7 47.7 %all-gather = s32[8,1,512]{2,1,0:T(1,128)S(1)} all-gather(s32[1,1,512]{2,1,0:T(1,128)S(1)} %bitcast.331), channel_id=1, replica_groups=mesh['rep'=1,'tp'=4,'sp'=8] {'sp'}, dimensions={0}, use_global_device_ids=true | all-gather | bytes 18432 | tf_op jit(solution)/shard_map/all_gather | solution.py:475
  91.7 0.2 copy.50
  92.1 0.4 fusion.99
  92.5 0.2 fusion.89
  92.7 0.3 fusion.45
  93.1 0.6 fusion.100
  93.7 0.4 fusion.21
  94.0 0.5 fusion.53
  94.6 0.8 fusion.101
  95.4 0.5 fusion.16
  95.9 0.7 fusion.81
  96.7 1.1 fusion.102
  97.8 0.6 fusion.10
  98.4 0.9 fusion.49
  99.3 1.3 fusion.103
  100.6 0.8 fusion.7
  101.4 1.1 fusion.75
  102.6 1.5 fusion.104
  104.1 1.3 fusion.6
  105.4 1.3 fusion.69
  106.7 1.8 fusion.105
  108.5 1.0 fusion.5
  109.5 1.5 fusion.63
  111.0 2.0 fusion.106
  113.0 1.2 fusion.4
  114.2 1.7 fusion.57
  115.9 1.3 copy.54
  117.2 9.0 %all-to-all-start.1 = ((bf16[8,512,1,128]{3,1,2,0:T(8,128)(2,1)}), bf16[8,512,1,128]{3,1,2,0:T(8,128)(2,1)S(1)}, u32[]{:S(2)}, u32[]{:S(2)}) async-start(bf16[8,512,1,128]{3,1,2,0:T(8,128)(2,1)} %bitcast.89), calls=%async_computation.1 | async-start | bytes 2097152 | tf_op jit(solution)/shard_map/all_to_all | solution.py:489
  126.2 8.5 %copy.74 = bf16[128,4,8,1280]{3,2,0,1:T(8,128)(2,1)} copy(bf16[128,4,8,1280]{3,2,1,0:T(8,128)(2,1)} %bitcast.302) | data formatting | bytes 20971520 | tf_op jit(solution)/shard_map/all_to_all | solution.py:491
  134.7 6.4 %all-to-all-done.1 = bf16[8,512,1,128]{3,1,2,0:T(8,128)(2,1)S(1)} async-done(((bf16[8,512,1,128]{3,1,2,0:T(8,128)(2,1)}), bf16[8,512,1,128]{3,1,2,0:T(8,128)(2,1)S(1)}, u32[]{:S(2)}, u32[]{:S(2)}) %all-to-all-start.1) | async-done | bytes 1048608 | tf_op jit(solution)/shard_map/all_to_all | solution.py:489
  141.1 6.1 %all-to-all-start.2 = ((bf16[1024,4,1280]{2,0,1:T(8,128)(2,1)}), bf16[1024,4,1280]{2,0,1:T(8,128)(2,1)}, u32[]{:S(2)}, u32[]{:S(2)}) async-start(bf16[1024,4,1280]{2,0,1:T(8,128)(2,1)} %bitcast.300), calls=%async_computation.2 | async-start | bytes 20971520 | tf_op jit(solution)/shard_map/all_to_all | solution.py:491
  147.1 0.2 all-gather.3.cloned.1.call-start
  147.4 0.7 copy.52
  148.1 1.2 copy.75
  149.4 147.8 %all-to-all-done.2 = bf16[1024,4,1280]{2,0,1:T(8,128)(2,1)} async-done(((bf16[1024,4,1280]{2,0,1:T(8,128)(2,1)}), bf16[1024,4,1280]{2,0,1:T(8,128)(2,1)}, u32[]{:S(2)}, u32[]{:S(2)}) %all-to-all-start.2) | async-done | bytes 10485792 | tf_op jit(solution)/shard_map/all_to_all | solution.py:491
  297.2 245.5 %mlp.1 = bf16[512,5120]{1,0:T(8,128)(2,1)} custom-call(bf16[512,4096]{1,0:T(8,128)(2,1)} %all-gather.3.cloned.1.call-done.attn, bf16[4096,1280]{1,0:T(8,128)(2,1)} %bitcast.93.wo, bf16[512,5120]{1,0:T(8,128)(2,1)} %x_hbm.1, f32[1,5120]{1,0:T(1,128)} %bitcast.330, bf16[5120,8192]{1,0:T(8,128)(2,1)} %wg.1, bf16[5120,8192]{1,0:T(8,128)(2,1)} %wu.1, ...), custom_call_target="tpu_custom_call" | custom-call | tf_op jit(solution)/shard_map/mlp/pallas_call | solution.py:442
  542.7 5.2 copy.84
  (53 shorter events, 1.4 us)
Async XLA Ops:
  7.2 5.1 copy-start.5
  37.5 6.1 %copy-start.4 = (s32[512]{0:T(512)S(1)}, s32[512]{0:T(512)}, u32[]{:S(2)}) copy-start(s32[512]{0:T(512)} %param.14) | copy-start | bytes 6148
  37.5 54.2 %all-to-all-start = ((bf16[512,8,3,128]{3,0,2,1:T(8,128)(2,1)}), bf16[512,8,3,128]{3,0,2,1:T(8,128)(2,1)S(1)}, u32[]{:S(2)}, u32[]{:S(2)}) async-start(bf16[512,8,3,128]{3,0,2,1:T(8,128)(2,1)} %pad_maximum_fusion), calls=%async_computation | async-start | bytes 6291456 | tf_op jit(solution)/shard_map/all_to_all | solution.py:474
  91.4 0.7 copy-start.2
  92.1 18.9 %copy-start.1 = (bf16[4096,1,128]{2,0,1:T(8,128)(2,1)}, bf16[4096,1,128]{2,0,1:T(8,128)(2,1)S(1)}, u32[]{:S(2)}) copy-start(bf16[4096,1,128]{2,0,1:T(8,128)(2,1)S(1)} %get-tuple-element.41) | copy-start | bytes 3145732
  92.1 22.1 %copy-start = (bf16[4096,1,128]{2,0,1:T(8,128)(2,1)}, bf16[4096,1,128]{2,0,1:T(8,128)(2,1)S(1)}, u32[]{:S(2)}) copy-start(bf16[4096,1,128]{2,0,1:T(8,128)(2,1)S(1)} %get-tuple-element.42) | copy-start | bytes 3145732
  92.1 1.0 slice-start
  95.9 0.7 slice-start.1
  101.4 1.1 slice-start.2
  109.5 1.5 copy-start.3
  117.2 23.9 %all-to-all-start.1 = ((bf16[8,512,1,128]{3,1,2,0:T(8,128)(2,1)}), bf16[8,512,1,128]{3,1,2,0:T(8,128)(2,1)S(1)}, u32[]{:S(2)}, u32[]{:S(2)}) async-start(bf16[8,512,1,128]{3,1,2,0:T(8,128)(2,1)} %bitcast.89), calls=%async_computation.1 | async-start | bytes 2097152 | tf_op jit(solution)/shard_map/all_to_all | solution.py:489
  141.1 156.1 %all-to-all-start.2 = ((bf16[1024,4,1280]{2,0,1:T(8,128)(2,1)}), bf16[1024,4,1280]{2,0,1:T(8,128)(2,1)}, u32[]{:S(2)}, u32[]{:S(2)}) async-start(bf16[1024,4,1280]{2,0,1:T(8,128)(2,1)} %bitcast.300), calls=%async_computation.2 | async-start | bytes 20971520 | tf_op jit(solution)/shard_map/all_to_all | solution.py:491
  147.1 150.1 %all-gather.3.cloned.1.call-start = ((), (), s32[]{:S(2)}) async-start(), calls=%async_computation.3 | async-start | bytes 5242880 | tf_op jit(solution)/shard_map/all_gather | solution.py:490
Sparse Core Ops, SparseCore 0:
  150.1 80.8 all-gather.2

commit v2 on v0

v2 whole, which is shorter than its diff:
```python
import functools

import jax
import jax.numpy as jnp
from jax import lax
from jax.experimental import pallas as pl
from jax.experimental.pallas import tpu as pltpu
from jax.sharding import PartitionSpec as P

HEAD_DIM = 128
ROPE_BASE = 500000.0
NORM_EPS = 1e-5
MESH = pl.DeviceIdType.MESH
BF16, F32 = jnp.bfloat16, jnp.float32
VMEM_BYTES = 63 * 2 ** 20
NIL, ONE, TWO, THREE, FOUR, EIGHT, SUB, LANES = 0, 1, 2, 3, 4, 8, 8, 128


def remote(src, dst, send_sem, recv_sem, to):
    return pltpu.make_async_remote_copy(src, dst, send_sem, recv_sem, device_id=to, device_id_type=MESH)


def start(copies):
    for c in copies:
        c.start()


def wait(copies):
    for c in copies:
        c.wait()


def top(n):
    return pl.ds(NIL, n)


def aligned(offset, n):
    return pl.ds(pl.multiple_of(offset, LANES), n)


def rope_tables(positions):
    half_dim = HEAD_DIM // 2
    inv_freq = jnp.power(jnp.float32(ROPE_BASE), -jnp.arange(half_dim, dtype=jnp.float32) * (2.0 / HEAD_DIM))
    angles = positions.astype(jnp.float32)[..., None] * inv_freq
    return jnp.cos(angles)[..., None, :], jnp.sin(angles)[..., None, :]


def front_kernel(heads, x_hbm, seg_row, rope_c, rope_s, gain, wq, wk, wv, wo,
                 kc, vc, attn, wo_g,
                 xu, wbuf, qb, kvb, sgb, fq, fk, m_b, l_b, acc, ao,
                 xsem, wsem, sg_s, sg_r, k1s, k1r, k2s, k2r, kps, kpr, w1s, w1r, w2s, w2r, w3s, w3r, wps, wpr,
                 a_l, a_s, a_r, h_s, h_r, csem):
    rows, dim = x_hbm.shape
    tp, sp = lax.axis_size("tp"), lax.axis_size("sp")
    hd = HEAD_DIM
    n_kv = wk.shape[ONE] // hd
    group = heads // n_kv
    wide = heads * hd
    col, wrow = dim // tp, wo.shape[NIL] // sp
    half = wrow // TWO
    y, s = lax.axis_index("tp"), lax.axis_index("sp")
    core, chip, n_chip = s % TWO, s // TWO, sp // TWO
    yp, ym = (y + ONE) % tp, (y + tp - ONE) % tp
    chip_at = lambda d: (chip + d) % n_chip * TWO
    up, dn, far = (chip_at(d) + core for d in (ONE, n_chip - ONE, TWO))
    pair = s + ONE - TWO * core
    to_pair, to_up, to_dn = ({"tp": y, "sp": d} for d in (pair, up, dn))
    to_p, to_m = ({"tp": d, "sp": s} for d in (yp, ym))
    scale2 = HEAD_DIM ** -0.5 * 1.4426950408889634

    kw = n_kv * hd
    n_x = xsem.shape[NIL]
    x_rows = rows // n_x
    x_copies = [pltpu.make_async_copy(x_hbm.at[pl.ds(i * x_rows, x_rows)], xu.at[pl.ds(i * x_rows, x_rows)], xsem.at[i])
                for i in range(n_x)]
    start(x_copies)
    kv_copies = [pltpu.make_async_copy(w, wbuf.at[NIL, :, pl.ds(i * kw, kw)], wsem.at[NIL, i]) for i, w in enumerate((wk, wv))]
    q_copies = [pltpu.make_async_copy(wq.at[:, pl.ds(t * TWO * kw, TWO * kw)], wbuf.at[ONE + t], wsem.at[ONE + t, NIL])
                for t in range(TWO)]

    barrier = pltpu.get_barrier_semaphore()
    for j in range(ONE, sp):
        pl.semaphore_signal(barrier, inc=ONE, device_id={"tp": y, "sp": (s + j) % sp}, device_id_type=MESH)
    for j in range(ONE, tp):
        pl.semaphore_signal(barrier, inc=ONE, device_id={"tp": (y + j) % tp, "sp": s}, device_id_type=MESH)

    def norm(i):
        x_copies[i].wait()
        step = x_rows // TWO

        @pl.loop(NIL, TWO)
        def _(j):
            rr = pl.ds(pl.multiple_of(i * x_rows + j * step, step), step)
            sq = jnp.zeros((step, LANES), F32)
            for b in range(dim // LANES):
                v = xu[rr, pl.ds(b * LANES, LANES)].astype(F32)
                sq += v * v
            inv = lax.rsqrt(jnp.sum(sq, axis=ONE, keepdims=True) * (1.0 / dim) + NORM_EPS)
            for b in range(dim // LANES):
                c = pl.ds(b * LANES, LANES)
                xu[rr, c] = (xu[rr, c].astype(F32) * inv * gain[:, c]).astype(BF16)

    norm(NIL)
    start(kv_copies)
    norm(ONE)
    pl.semaphore_wait(barrier, sp + tp - TWO)

    def w1(j):
        rank, mine = (y + j) % tp, aligned(s * wrow, wrow)
        return remote(wo.at[mine, aligned(rank * col, col)], wo_g.at[tp - ONE - j, mine],
                      w1s.at[j - ONE], w1r.at[tp - ONE - j], {"tp": rank, "sp": s})

    def sg(j):
        return remote(seg_row, sgb.at[s], sg_s.at[j], sg_r.at[j], {"tp": y, "sp": (s + j) % sp})

    for j in range(ONE, sp):
        sg(j).start()
    for j in range(ONE, tp):
        w1(j).start()

    def w_blk(dev, r0, n):
        return wo_g.at[:, pl.ds(pl.multiple_of(dev * wrow + r0, half), n)]

    def w2(side):
        b = w_blk(s, NIL, wrow)
        return remote(b, b, w2s.at[side], w2r.at[ONE - side], (to_up, to_dn)[side])

    def w3(side):
        b = w_blk((up, dn)[side], (half, NIL)[side], half)
        return remote(b, b, w3s.at[side], w3r.at[side], (to_dn, to_up)[side])

    def wp(j):
        b = w_blk((s, up, dn, far)[j], NIL, wrow)
        return remote(b, b, wps.at[j], wpr.at[j], to_pair)

    start(q_copies)
    for i in range(TWO, n_x):
        norm(i)

    def rope(t):
        return (t * rope_c[...] + pltpu.roll(t, hd // TWO, ONE) * rope_s[...]).astype(BF16)

    wait(kv_copies)
    r = jnp.dot(xu[...], wbuf[NIL], preferred_element_type=F32)
    for g in range(n_kv):
        kvb[s, TWO * g] = rope(r[:, g * hd:(g + ONE) * hd])
        kvb[s, TWO * g + ONE] = r[:, kw + g * hd:kw + (g + ONE) * hd].astype(BF16)

    def k_blk(dev, g, lo=NIL, n=TWO):
        return kvb.at[dev, pl.ds(TWO * g + lo, n)]

    def k1(g, side):
        b = k_blk(s, g)
        return remote(b, b, k1s.at[g, side], k1r.at[g, ONE - side], (to_up, to_dn)[side])

    def k2(g, side):
        b = k_blk((up, dn)[side], g, ONE - side, ONE)
        return remote(b, b, k2s.at[g, side], k2r.at[g, side], (to_dn, to_up)[side])

    def kp(g, j):
        b = k_blk((s, up, dn, far)[j], g)
        return remote(b, b, kps.at[g, j], kpr.at[g, j], to_pair)

    def k_start(g):
        k1(g, NIL).start()
        k1(g, ONE).start()
        kp(g, NIL).start()

    def k_mid(g):
        for side in range(TWO):
            k1(g, ONE - side).wait_recv()
            k2(g, side).start()
            kp(g, ONE + side).start()

    def k_last(g):
        k2(g, NIL).wait_recv()
        k2(g, ONE).wait_recv()
        kp(g, THREE).start()

    k_start(NIL)

    for t in range(TWO):
        q_copies[t].wait()
        r = jnp.dot(xu[...], wbuf[ONE + t], preferred_element_type=F32)
        for g in range(heads // TWO):
            qb[t * (heads // TWO) + g] = rope(r[:, g * hd:(g + ONE) * hd])

    for j in range(ONE, sp):
        sg(j).wait_recv()
    sgb[s] = seg_row[...]
    lane = lax.broadcasted_iota(jnp.int32, (rows, LANES), ONE).astype(F32)

    def seg_col(dev):
        return jnp.broadcast_to(sgb[dev, top(ONE), :], (LANES, rows)).T

    fq[...] = jnp.where(seg_col(s) == lane, 1.0, 0.0).astype(BF16)

    @pl.loop(NIL, sp)
    def _(b):
        fk[b] = jnp.where(seg_col(b) == lane, 0.0, -1e30).astype(BF16)

    def attend(h, g, b0, nb, own):
        nk = nb * rows
        q = jnp.concatenate([qb[h], fq[...]], axis=ONE)
        k = jnp.concatenate([kvb[pl.ds(b0, nb), TWO * g].reshape(nk, hd), fk[pl.ds(b0, nb)].reshape(nk, LANES)], axis=ONE)
        v = kvb[pl.ds(b0, nb), TWO * g + ONE].reshape(nk, hd)
        sc = lax.dot_general(q, k, (((ONE,), (ONE,)), ((), ())), preferred_element_type=F32)
        if own:
            lo = nk - rows
            i, j = (lax.broadcasted_iota(jnp.int32, (rows, rows), d) for d in range(TWO))
            tail = jnp.where(i >= j, sc[:, lo:], -1e30)
            sc = jnp.concatenate([sc[:, :lo], tail], axis=ONE) if lo else tail
        mx = jnp.max(sc, axis=ONE, keepdims=True)
        if own:
            mn = jnp.broadcast_to(mx, (rows, LANES))
        else:
            mn = jnp.maximum(m_b[h], mx)
            al = jnp.exp2((m_b[h] - mn) * scale2)
        ps = [jnp.exp2((sc[:, j * LANES:(j + ONE) * LANES] - mn) * scale2) for j in range(nk // LANES)]
        ls = functools.reduce(jnp.add, ps)
        o = jnp.dot(jnp.concatenate([p.astype(BF16) for p in ps], axis=ONE), v, preferred_element_type=F32)
        m_b[h] = mn
        if own:
            l_b[h], acc[h] = ls, o
        else:
            l_b[h] = l_b[h] * al + ls
            acc[h] = acc[h] * al + o

    def a_at(rank, h, r0, n):
        return attn.at[pl.ds(r0, n), aligned(rank * wide + h * hd, hd)]

    def a1(h, side):
        return remote(ao.at[h], a_at(y, h, NIL, rows), a_s.at[side, h], a_r.at[ONE - side, h], (to_p, to_m)[side])

    def a2(h, side):
        b = a_at((yp, ym)[side], h, (rows // TWO, NIL)[side], rows // TWO)
        return remote(b, b, h_s.at[side, h], h_r.at[side, h], (to_m, to_p)[side])

    def a_own(h):
        return pltpu.make_async_copy(ao.at[h], a_at(y, h, NIL, rows), a_l.at[h])

    def pass_on(h):
        for side in range(TWO):
            a1(h, ONE - side).wait_recv()
            a2(h, side).start()

    @pl.loop(NIL, n_kv)
    def _(g):
        @pl.when(g == NIL)
        def _():
            k_mid(NIL)
            k_start(ONE)

        kp(g, NIL).wait_recv()

        @pl.loop(NIL, group)
        def _(i):
            @pl.when(core == NIL)
            def _():
                attend(g * group + i, g, s, ONE, True)

            @pl.when(core == ONE)
            def _():
                attend(g * group + i, g, chip_at(NIL), TWO, True)

        k_last(g)
        for j in range(ONE, FOUR):
            kp(g, j).wait_recv()

        @pl.loop(NIL, group)
        def _(i):
            h = g * group + i

            @pl.when(chip >= ONE)
            def _():
                attend(h, g, chip_at(n_chip - ONE), TWO, False)

            @pl.when(chip == n_chip - ONE)
            def _():
                attend(h, g, chip_at(ONE), TWO, False)

            @pl.when(chip >= TWO)
            def _():
                attend(h, g, chip_at(TWO), TWO, False)

            ao[h] = (acc[h] / jnp.sum(l_b[h], axis=ONE, keepdims=True)).astype(BF16)
            a1(h, NIL).start()
            a1(h, ONE).start()
            a_own(h).start()

            @pl.when(h == ONE)
            def _():
                k_mid(ONE)
                for j in range(ONE, tp):
                    w1(j).wait_recv()
                w2(NIL).start()
                w2(ONE).start()
                wp(NIL).start()

            @pl.when(h >= TWO)
            def _():
                pass_on(h - TWO)

    mine_kv = s // (sp // n_kv)
    caches = [pltpu.make_async_copy(kvb.at[:, TWO * mine_kv + i], c, csem.at[i]) for i, c in enumerate((kc, vc))]
    start(caches)
    pass_on(heads - TWO)
    for side in range(TWO):
        w2(ONE - side).wait_recv()
        w3(side).start()
        wp(ONE + side).start()
    pass_on(heads - ONE)
    w3(NIL).wait_recv()
    w3(ONE).wait_recv()
    wp(THREE).start()

    @pl.loop(NIL, heads)
    def _(h):
        for side in range(TWO):
            a2(h, side).wait_recv()
            a1(h, side).wait_send()
            a2(h, side).wait_send()
        a_own(h).wait()

    for j in range(FOUR):
        wp(j).wait_recv()
        wp(j).wait_send()
        for g in range(n_kv):
            kp(g, j).wait_send()
    for side in range(TWO):
        w2(side).wait_send()
        w3(side).wait_send()
        for g in range(n_kv):
            k1(g, side).wait_send()
            k2(g, side).wait_send()
    for j in range(ONE, tp):
        w1(j).wait_send()
    for j in range(ONE, sp):
        sg(j).wait_send()
    wait(caches)


def front_call(x_in, positions, segments, gain, wq, wk, wv, wo):
    rows, dim = x_in.shape
    tp, sp = lax.axis_size("tp"), lax.axis_size("sp")
    heads, n_kv = wq.shape[ONE] // HEAD_DIM, wk.shape[ONE] // HEAD_DIM
    cos_t, sin_t = (t[:, NIL] for t in rope_tables(positions))
    rope_c = jnp.concatenate([cos_t, cos_t], axis=ONE)
    rope_s = jnp.concatenate([-sin_t, sin_t], axis=ONE)
    seg_row = jnp.broadcast_to(segments.astype(F32), (SUB, rows))
    dma = pltpu.SemaphoreType.DMA
    hbm, vmem = pl.BlockSpec(memory_space=pl.ANY), pl.BlockSpec(memory_space=pltpu.VMEM)
    kv_shape = jax.ShapeDtypeStruct((sp, rows, HEAD_DIM), BF16)
    per_head, stat = (heads, rows, HEAD_DIM), ((heads, rows, LANES), F32)
    bufs = [((rows, dim), BF16), ((THREE, dim, TWO * n_kv * HEAD_DIM), BF16), (per_head, BF16),
            ((sp, TWO * n_kv, rows, HEAD_DIM), BF16), ((sp, SUB, rows), F32), ((rows, LANES), BF16), ((sp, rows, LANES), BF16),
            stat, stat, stat, (per_head, BF16)]
    sems = [(FOUR,), (THREE, TWO), (sp,), (sp,)] + [(n_kv, TWO)] * FOUR + [(n_kv, FOUR)] * TWO + [(tp - ONE,)] * TWO
    sems += [(TWO,)] * FOUR + [(FOUR,)] * TWO + [(heads,)] + [(TWO, heads)] * FOUR + [(TWO,)]
    return pl.pallas_call(
        functools.partial(front_kernel, heads), name="front",
        out_shape=[kv_shape, kv_shape, jax.ShapeDtypeStruct((rows, tp * heads * HEAD_DIM), BF16),
                   jax.ShapeDtypeStruct((tp - ONE, wo.shape[NIL], dim // tp), BF16)],
        in_specs=[hbm] + [vmem] * FOUR + [hbm] * FOUR, out_specs=[hbm] * FOUR,
        scratch_shapes=[pltpu.VMEM(*b) for b in bufs] + [dma(q) for q in sems],
        compiler_params=pltpu.CompilerParams(collective_id=TWO, has_side_effects=True, vmem_limit_bytes=VMEM_BYTES),
    )(x_in, seg_row, rope_c, rope_s, gain.reshape(ONE, dim), wq, wk, wv, wo)


def mlp_kernel(chunks, cb, plan, attn, wo, wo_g, x_hbm, gain, wg, wu, wd, y_hbm,
               wbuf, hbuf, xmid, srow, sin, p_own, p_out, d_in, f_in, e_in, ystage, *rest):
    n_ch = len(chunks)
    u2 = rest[:n_ch]
    (wsem, asem, xsem, s_s, s_r, u1s, u1r, u2s, u2r, ups, upr,
     d_s, d_r, f_s, f_r, e_s, e_r, a_l, a_s, a_r, h_s, h_r) = rest[n_ch:]
    rows, dim = x_hbm.shape
    depth = attn.shape[ONE]
    tp = lax.axis_size("tp")
    col = dim // tp
    nb = col // cb
    wide = TWO * cb
    ff = wg.shape[ONE] // TWO
    slots = wbuf.shape[NIL]
    y, s = lax.axis_index("tp"), lax.axis_index("sp")
    core = s % TWO
    pair = s + ONE - TWO * core
    yp, ym, y2 = (y + ONE) % tp, (y + tp - ONE) % tp, (y + TWO) % tp
    to_pair, to_p, to_m, to_2 = ({"tp": y, "sp": pair}, {"tp": yp, "sp": s}, {"tp": ym, "sp": s}, {"tp": y2, "sp": s})
    starts = [sum(chunks[:i]) for i in range(n_ch)]
    n_g, n_d = ff // wide, nb * tp // FOUR

    def cols(block, width):
        return aligned(block * width, width)

    n_o = -(-col // wide)
    part = depth // tp

    def o_width(t):
        return min(wide, col - t * wide)

    def o_tile(t):
        w = o_width(t)
        srcs = [wo.at[:, aligned(y * col + t * wide, w)]] + [wo_g.at[j, :, pl.ds(t * wide, w)] for j in range(tp - ONE)]
        return [pltpu.make_async_copy(src, wbuf.at[t, aligned((y + j) % tp * part, part), top(w)], wsem.at[t, j])
                for j, src in enumerate(srcs)]

    def g_tile(n, slot):
        c = aligned(core * ff + n * cb, cb)
        return [pltpu.make_async_copy(w.at[:, c], wbuf.at[slot, :, pl.ds(i * cb, cb)], wsem.at[slot, i])
                for i, w in enumerate((wg, wu))]

    def d_cols(m):
        q = m // nb
        d = (TWO + THREE * q + THREE * (q * (q - ONE) // TWO)) % FOUR
        return aligned((y + d) % tp * col + m % nb * cb, cb)

    def d_tile(p, slot):
        return [pltpu.make_async_copy(wd.at[aligned(core * ff, ff), d_cols(TWO * p + i)],
                                      wbuf.at[slot, top(ff), pl.ds(i * cb, cb)], wsem.at[slot, i]) for i in range(TWO)]

    def two(tile, j, base):
        return [c for i in range(TWO) for c in tile(TWO * j + i, (base + TWO * j + i) % slots)]

    a_copy = pltpu.make_async_copy(attn, hbuf.at[top(rows), top(depth)], asem)
    x_copies = [pltpu.make_async_copy(x_hbm.at[pl.ds(r0, r), cols(y, col)], u2[i].at[top(r), cols(y, col)], xsem.at[i])
                for i, (r0, r) in enumerate(zip(starts, chunks))]
    a_copy.start()
    for t in range(n_o):
        start(o_tile(t))
        if not t:
            start(x_copies)
    base = n_o
    start(g_tile(NIL, base))

    barrier = pltpu.get_barrier_semaphore()
    for to in (to_pair, to_p, to_m, to_2):
        pl.semaphore_signal(barrier, inc=ONE, device_id=to, device_id_type=MESH)
    pl.semaphore_wait(barrier, FOUR)

    step = rows // TWO

    def stat(j, i):
        to = (to_p, to_m, to_2)[i]
        return remote(srow.at[j], sin.at[j, i], s_s.at[j, i], s_r.at[j, i], to)

    a_copy.wait()
    wait(x_copies)
    for j in range(TWO):
        for t in range(n_o):
            w = o_width(t)
            if not j:
                wait(o_tile(t))
            xmid[pl.ds(j * step, step), pl.ds(t * wide, w)] = jnp.dot(
                hbuf[pl.ds(j * step, step), top(depth)], wbuf[t, top(depth), top(w)], preferred_element_type=F32)
            if j and not t:
                start(g_tile(ONE, NIL))
        for i, (r0, r) in enumerate(zip(starts, chunks)):
            lo, hi = max(r0, j * step), min(r0 + r, j * step + step)
            if lo < hi:
                xmid[pl.ds(lo, hi - lo), :] += u2[i][pl.ds(lo - r0, hi - lo), cols(y, col)].astype(F32)
        sq = jnp.zeros((step, LANES), F32)
        for b in range(col // LANES):
            v = xmid[pl.ds(j * step, step), pl.ds(b * LANES, LANES)]
            sq += v * v
        srow[j] = jnp.broadcast_to(jnp.sum(sq, axis=ONE, keepdims=True), (step, LANES)).T[:SUB, :]
        for i in range(tp - ONE):
            stat(j, i).start()

    def inverse(j):
        for i in range(tp - ONE):
            stat(j, i).wait()
        tot = srow[j]
        for i in range(tp - ONE):
            tot += sin[j, i]
        inv = lax.rsqrt(tot * (1.0 / dim) + NORM_EPS)
        return jnp.broadcast_to(inv[:ONE, :], (LANES, step)).T

    def norm_rows(j, inv_col):
        for i, (r0, r) in enumerate(zip(starts, chunks)):
            lo, hi = max(r0, j * step), min(r0 + r, j * step + step)
            if lo < hi:
                for b in range(col // LANES):
                    c = aligned(y * col + b * LANES, LANES)
                    u2[i][pl.ds(lo - r0, hi - lo), c] = (xmid[pl.ds(lo, hi - lo), pl.ds(b * LANES, LANES)]
                                                         * inv_col[lo - j * step:hi - j * step, :] * gain[:, c]).astype(BF16)

    def u_blk(i, row0, n_rows, rank):
        return u2[i].at[pl.ds(row0, n_rows), cols(rank, col)]

    def u_first(i, side):
        b = u_blk(i, NIL, chunks[i], y)
        return remote(b, b, u1s.at[i, side], u1r.at[i, ONE - side], (to_p, to_m)[side])

    def u_second(i, side):
        h = chunks[i] // TWO
        b = u_blk(i, h, h, yp) if side == NIL else u_blk(i, NIL, h, ym)
        return remote(b, b, u2s.at[i, side], u2r.at[i, side], (to_m, to_p)[side])

    def u_pair(i, j):
        r, rank = chunks[i], (y, yp, ym, y2)[j]
        return remote(u_blk(i, NIL, r, rank), u_blk(i, r, r, rank), ups.at[i, j], upr.at[i, j], to_pair)

    def u_start(i):
        u_first(i, NIL).start()
        u_first(i, ONE).start()
        u_pair(i, NIL).start()

    def u_mid(i):
        for side in range(TWO):
            u_first(i, ONE - side).wait_recv()
            u_second(i, side).start()
            u_pair(i, ONE + side).start()

    def u_last(i):
        for side in range(TWO):
            u_second(i, side).wait_recv()
        u_pair(i, THREE).start()

    def u_ready(i):
        for j in range(FOUR):
            u_pair(i, j).wait_recv()

    def u_drain(i):
        for side in range(TWO):
            u_first(i, side).wait_send()
            u_second(i, side).wait_send()
        for j in range(FOUR):
            u_pair(i, j).wait_send()

    def d_copy(i, m, slot):
        r, par = chunks[i], i % TWO
        return remote(p_out.at[slot, top(r)], d_in.at[par, m, top(r)], d_s.at[slot], d_r.at[par, m], to_pair)

    def t_add(i, m):
        r, par = chunks[i], i % TWO
        d_copy(i, m, NIL).wait_recv()
        p_own[m, top(r)] += d_in[par, m, top(r)]

    def f_copy(i, k, side):
        h, par = chunks[i] // TWO, i % TWO
        return remote(p_own.at[k, pl.ds(side * h, h)], f_in.at[par, side, k, top(h)],
                      f_s.at[side, k], f_r.at[par, side, k], (to_m, to_p)[side])

    def t_f(i, k):
        f_copy(i, k, NIL).start()
        f_copy(i, k, ONE).start()

    def e_copy(i, k, side):
        r, par = chunks[i], i % TWO
        return remote(p_own.at[(TWO - side) * nb + k, top(r)], e_in.at[par, side, k, top(r)],
                      e_s.at[side, k], e_r.at[par, side, k], (to_m, to_p)[side])

    def t_e(i, k, side):
        h, par = chunks[i] // TWO, i % TWO
        f_copy(i, k, side).wait_recv()
        p_own[(TWO - side) * nb + k, pl.ds(side * h, h)] += f_in[par, side, k, top(h)]
        e_copy(i, k, side).start()

    def y_at(i, row0, n_rows, rank, k):
        return y_hbm.at[pl.ds(starts[i] + row0, n_rows), aligned(rank * col + k * cb, cb)]

    def a_copy_y(i, k, side):
        r, par = chunks[i], i % TWO
        return remote(ystage.at[par, k, top(r)], y_at(i, NIL, r, y, k), a_s.at[par, side, k], a_r.at[par, ONE - side, k],
                      (to_p, to_m)[side])

    def a_local(i, k):
        r, par = chunks[i], i % TWO
        return pltpu.make_async_copy(ystage.at[par, k, top(r)], y_at(i, NIL, r, y, k), a_l.at[par, k])

    def h_copy(i, k, side):
        h = chunks[i] // TWO
        b = y_at(i, h, h, yp, k) if side == NIL else y_at(i, NIL, h, ym, k)
        return remote(b, b, h_s.at[i, side, k], h_r.at[i, side, k], (to_m, to_p)[side])

    def t_final(i, k):
        r, par = chunks[i], i % TWO
        for side in range(TWO):
            e_copy(i, k, side).wait_recv()
        v = (p_own[THREE * nb + k, top(r)] + e_in[par, NIL, k, top(r)] + e_in[par, ONE, k, top(r)]
             + xmid[pl.ds(starts[i], r), pl.ds(k * cb, cb)])
        ystage[par, k, top(r)] = v.astype(BF16)
        for side in range(TWO):
            a_copy_y(i, k, side).start()
        a_local(i, k).start()

    def t_fwd(i, k):
        for side in range(TWO):
            a_copy_y(i, k, ONE - side).wait_recv()
            h_copy(i, k, side).start()

    def sums_sent(i):
        for k in range(nb):
            for side in range(TWO):
                f_copy(i, k, side).wait_send()
                e_copy(i, k, side).wait_send()

    def rows_done(i):
        for k in range(nb):
            for side in range(TWO):
                h_copy(i, k, side).wait_recv()
                h_copy(i, k, side).wait_send()
                a_copy_y(i, k, side).wait_send()
            a_local(i, k).wait()

    norm_rows(NIL, inverse(NIL))
    u_start(NIL)
    norm_rows(ONE, inverse(ONE))
    u_mid(NIL)
    u_start(ONE)
    u_last(NIL)
    u_ready(NIL)

    tasks = {"mid": u_mid, "last": u_last, "start": u_start, "e": t_e, "final": t_final, "fwd": t_fwd}

    def run(todo, at):
        for when, name, *args in todo:
            @pl.when(at == when)
            def _():
                tasks[name](*args)

    for i in range(n_ch):
        r = chunks[i]
        g_base, d_base = base % slots, (base + TWO * n_g) % slots
        base += TWO * (n_g + n_d)

        @pl.loop(NIL, n_g)
        def _(j):
            @pl.when(j + ONE < n_g)
            def _():
                start(two(g_tile, j + ONE, g_base))

            @pl.when(j + ONE >= n_g)
            def _():
                start(two(d_tile, NIL, d_base))

            wait(two(g_tile, j, g_base))
            for q in range(TWO):
                n = TWO * j + q
                g = jnp.dot(u2[i][...], wbuf[(g_base + n) % slots], preferred_element_type=F32)
                hbuf[top(TWO * r), aligned(n * cb, cb)] = (jax.nn.silu(g[:, :cb]) * g[:, cb:]).astype(BF16)
            run(plan[i][NIL], j)

        if i:
            sums_sent(i - ONE)

        @pl.loop(NIL, n_d)
        def _(p):
            @pl.when(p + ONE < n_d)
            def _():
                start(two(d_tile, p + ONE, d_base))

            if i + ONE < n_ch:
                @pl.when(p + ONE >= n_d)
                def _():
                    start(two(g_tile, NIL, base % slots))

            wait(two(d_tile, p, d_base))
            out = p % TWO * FOUR

            @pl.when(p >= TWO)
            def _():
                for q in range(FOUR):
                    d_copy(i, q, out + q).wait_send()

            for q in range(TWO):
                v = jnp.dot(hbuf[top(TWO * r), top(ff)], wbuf[(d_base + TWO * p + q) % slots, top(ff)],
                            preferred_element_type=F32)
                for e in range(TWO):
                    b = TWO * q + e
                    p_own[FOUR * p + b, top(r)] = v[:r, e * cb:(e + ONE) * cb]
                    p_out[out + b, top(r)] = v[r:, e * cb:(e + ONE) * cb]
            for q in range(FOUR):
                d_copy(i, FOUR * p + q, out + q).start()

            @pl.when(p >= ONE)
            def _():
                for q in range(FOUR):
                    t_add(i, FOUR * (p - ONE) + q)

            @pl.when(p == ONE)
            def _():
                for k in range(FOUR):
                    t_f(i, k)

            @pl.when(p == TWO)
            def _():
                for k in range(FOUR, nb):
                    t_f(i, k)
            run(plan[i][ONE], p)

        for q in range(FOUR):
            t_add(i, FOUR * (n_d - ONE) + q)
        for q in range(FOUR):
            for out in range(TWO):
                d_copy(i, q, FOUR * out + q).wait_send()
        for name, *args in plan[i][TWO]:
            tasks[name](*args)
        if i + ONE < n_ch:
            u_ready(i + ONE)

    last = n_ch - ONE
    if last >= TWO:
        rows_done(last - TWO)
    for k in range(nb):
        t_final(last, k)
        if k >= TWO:
            t_fwd(last, k - TWO)
    for k in range(nb - TWO, nb):
        t_fwd(last, k)
    for i in range(max(last - ONE, NIL), n_ch):
        rows_done(i)
    sums_sent(last)
    for i in range(n_ch):
        u_drain(i)


CHUNKS = (192, 192, 128)


def mlp_plan():
    early = lambda i: [(3, "e", i, 0, 1), (3, "e", i, 1, 1), (4, "e", i, 2, 1), (4, "e", i, 0, 0), (4, "e", i, 1, 0)]
    late = lambda i: [("e", i, 3, 1), ("e", i, 2, 0), ("e", i, 4, 1), ("e", i, 3, 0), ("e", i, 4, 0)]
    at_start = lambda i: [(0, *t) for t in late(i)]
    finals = lambda i, at: [(a, "final", i, k) for k, a in enumerate(at)]
    passed = lambda i, at: [(a, "fwd", i, k) for k, a in enumerate(at)]
    gather = [(1, "mid", 1), (1, "start", 2), (3, "last", 1), (4, "mid", 2), (6, "last", 2)]
    return ((gather, early(0), ()),
            (at_start(0) + finals(0, (1, 2, 3, 4, 5)) + passed(0, (5, 6, 6, 6, 7)), early(1), ()),
            (at_start(1) + finals(1, (2, 3, 4, 6, 7)), passed(1, (0, 1, 1, 2, 2)) + early(2), late(2)))


def mlp_call(attn, wo, wo_g, x_in, gain, wg, wu, wd):
    rows, dim = x_in.shape
    tp = lax.axis_size("tp")
    cb = TWO * LANES
    nb = dim // tp // cb
    col, ff = nb * cb, wg.shape[ONE] // TWO
    n_ch, rm = len(CHUNKS), max(CHUNKS)
    dma = pltpu.SemaphoreType.DMA
    two_two, par_two = [(n_ch, TWO)] * FOUR + [(n_ch, FOUR)] * TWO, (TWO, TWO, nb)
    sems = [(FOUR, tp), (), (n_ch,), (TWO, tp - ONE), (TWO, tp - ONE), *two_two, (EIGHT,), (TWO, tp * nb),
            (TWO, nb), par_two, (TWO, nb), par_two, (TWO, nb), par_two, par_two, (n_ch, TWO, nb), (n_ch, TWO, nb)]
    bufs = [((FOUR, dim, TWO * cb), BF16), ((max(rows, TWO * rm), max(ff, attn.shape[ONE])), BF16), ((rows, col), F32),
            ((TWO, SUB, rows // TWO), F32), ((TWO, tp - ONE, SUB, rows // TWO), F32), ((tp * nb, rm, cb), F32),
            ((EIGHT, rm, cb), F32), ((TWO, tp * nb, rm, cb), F32), ((TWO, TWO, nb, rm // TWO, cb), F32),
            ((TWO, TWO, nb, rm, cb), F32), ((TWO, nb, rm, cb), BF16), *[((TWO * r, dim), BF16) for r in CHUNKS]]
    hbm = pl.BlockSpec(memory_space=pl.ANY)
    return pl.pallas_call(
        functools.partial(mlp_kernel, CHUNKS, cb, mlp_plan()), name="mlp",
        out_shape=jax.ShapeDtypeStruct((rows, dim), BF16),
        in_specs=[hbm, hbm, hbm, hbm, pl.BlockSpec(memory_space=pltpu.VMEM), hbm, hbm, hbm], out_specs=hbm,
        scratch_shapes=[pltpu.VMEM(*b) for b in bufs] + [dma(q) for q in sems],
        compiler_params=pltpu.CompilerParams(collective_id=ONE, has_side_effects=True, vmem_limit_bytes=VMEM_BYTES),
    )(attn, wo, wo_g, x_in, gain.reshape(ONE, dim), wg, wu, wd)


def solution(mesh):
    row_spec = P(("rep", "sp"), None)
    tok_spec = P(("rep", "sp"))
    full_spec = P(None)
    col_spec = P(None, "tp")
    wrow_spec = P("tp", None)
    cache_spec = P("rep", ("tp", "sp"), None)

    def local_layer(x_in, positions, segments, gain_attn, w_q, w_k, w_v, w_o, gain_mlp, w_gate, w_up, w_down):
        kc, vc, attn, wo_g = front_call(x_in, positions, segments, gain_attn, w_q, w_k, w_v, w_o)
        y_out = mlp_call(attn, w_o, wo_g, x_in, gain_mlp, w_gate, w_up, w_down)
        return y_out, kc.reshape(-1, 1, HEAD_DIM), vc.reshape(-1, 1, HEAD_DIM)

    return jax.shard_map(local_layer, mesh=mesh,
                         in_specs=(row_spec, tok_spec, tok_spec, full_spec, col_spec, col_spec, col_spec, wrow_spec,
                                   full_spec, col_spec, col_spec, wrow_spec),
                         out_specs=(row_spec, cache_spec, cache_spec), check_vma=False)
```

time: 739 us -> 316 us (0.43); the launches traced: 730 us -> 316 us
  waiting for transfers between devices: 379 us -> 0 us
  Pallas kernels: 0 us -> 304 us
  matrix products: 210 us -> 0 us
  blocking collectives: 71.1 us -> 0 us
  other arithmetic: 42.9 us -> 3.37 us
  between operations: 15 us -> 0.68 us
    psum x2 -> x0, waiting for transfers between devices: 379 us -> none  [the longest x1 190 us: local_layer(): lax.psum(jnp.dot(attn_local, w_o, preferred_element_type=jnp.float32), 'tp')]
    pallas_call x0 -> x2, Pallas kernels: none -> 304 us  [the longest x1 225 us: mlp_call(): pl.pallas_call(functools.partial(mlp_kernel, CHUNKS, cb, mlp_plan()), nam...]
    dot_general x23 -> x0, matrix products: 210 us -> none  [the longest x1 58 us: mlp_tail(): up_act = jnp.dot(u_mlp, w_up, preferred_element_type=jnp.float32)]
    all_gather x1 -> x0, blocking collectives: 47.9 us -> none  [local_layer(): seg_all = lax.all_gather(segments, 'sp', tiled=True)]
    all_to_all x1 -> x0, blocking collectives: 23.2 us -> none  [local_layer(): lax.all_to_all(attn_heads, 'sp', 0, 2, tiled=True)]
    convert_element_type x2 -> x1, other arithmetic: 22 us -> 0.68 us  [front_call(): seg_row = jnp.broadcast_to(segments.astype(F32), (SUB, rows))]
    reduce_sum x10 -> x0, other arithmetic: 16.5 us -> none  [the longest x2 10.5 us: rms_norm(): mean_sq = jnp.mean(x_f32 * x_f32, axis=-1, keepdims=True)]
  transfers between devices with their start and end apart: 3 -> 0, of which waited for: 2 -> 0; matrix products, arithmetic and copies ran while one was open for 0% -> 0% of each run, Pallas kernels for 0% -> 0%
where the time goes in v2:
time: 316 us
  Pallas kernels  304 us (96%)
  local copies, waits for them, and re-layouts  7.89 us (2%)
  other arithmetic  3.37 us (1%)
    pallas_call x1, Pallas kernels, mlp_call(): pl.pallas_call(functools.partial(mlp_kernel, CHUNKS, cb, mlp_plan()), nam...  225 us
    pallas_call x1, Pallas kernels, front_call(): pl.pallas_call(functools.partial(front_kernel, heads), name='front', out_...  78.5 us
    unnamed x7, local copies, waits for them, and re-layouts  7.28 us

profile of v2, /device:TPU:97, one launch (start us, length us, event | category | flops | bytes accessed | tf_op | source)
XLA Modules:
  0.0 315.6 jit_solution(18331691130555844595)
XLA Ops:
  0.6 0.7 convert_element_type.7
  1.3 0.7 convert_element_type.6
  2.0 0.6 broadcast_in_dim.2.seg_row
  2.6 1.0 fusion
  3.6 1.0 pad_maximum_fusion
  4.6 78.5 %front.1 = (bf16[8,512,128]{2,1,0:T(8,128)(2,1)}, bf16[8,512,128]{2,1,0:T(8,128)(2,1)}, bf16[512,4096]{1,0:T(8,128)(2,1)}, bf16[3,1024,1280]{2,1,0:T(8,128)(2,1)}) custom-call(bf16[512,5120]{1,0:T(8,128)(2,1)} %x_hbm.3, f32[8,512]{1,0:T(8,128)} %broadcast_in_dim.2.seg_row, f32[512,128]{1,0:T(8,128)} %get-tuple-element.14.rope_c, ...), custom_call_target="tpu_custom_call" | custom-call | tf_op jit(solution)/shard_map/front/pallas_call | solution.py:360
  83.2 225.1 %mlp.1 = bf16[512,5120]{1,0:T(8,128)(2,1)} custom-call(bf16[512,4096]{1,0:T(8,128)(2,1)} %get-tuple-element.7.attn, bf16[1024,5120]{1,0:T(8,128)(2,1)} %wo.3, bf16[3,1024,1280]{2,1,0:T(8,128)(2,1)} %get-tuple-element.8.wo_g, bf16[512,5120]{1,0:T(8,128)(2,1)} %x_hbm.3, f32[1,5120]{1,0:T(1,128)} %bitcast.7, bf16[5120,8192]{1,0:T(8,128)(2,1)} %wg.1, ...), custom_call_target="tpu_custom_call" | custom-call | tf_op jit(solution)/shard_map/mlp/pallas_call | solution.py:749
  308.3 0.0 copy-start.1
  308.3 0.0 copy-start
  308.3 5.3 %copy.18 = bf16[512,5120]{1,0:T(8,128)(2,1)} copy(bf16[512,5120]{1,0:T(8,128)(2,1)} %mlp.1) | data formatting | bytes 10485760
  313.7 0.0 copy-done.1
  313.7 1.0 copy.19
  314.6 0.0 copy-done
  314.6 1.0 copy.20
  (1 shorter events, 0.0 us)
Async XLA Ops:
  308.3 5.4 %copy-start.1 = (bf16[8,512,128]{2,1,0:T(8,128)(2,1)S(1)}, bf16[8,512,128]{2,1,0:T(8,128)(2,1)}, u32[]{:S(2)}) copy-start(bf16[8,512,128]{2,1,0:T(8,128)(2,1)} %get-tuple-element.9) | copy-start | bytes 3145732
  308.3 6.3 %copy-start = (bf16[8,512,128]{2,1,0:T(8,128)(2,1)S(1)}, bf16[8,512,128]{2,1,0:T(8,128)(2,1)}, u32[]{:S(2)}) copy-start(bf16[8,512,128]{2,1,0:T(8,128)(2,1)} %get-tuple-element.10) | copy-start | bytes 3145732

commit v3 on v2

v3 whole, which is shorter than its diff:
```python
import functools

import jax
import jax.numpy as jnp
from jax import lax
from jax.experimental import pallas as pl
from jax.experimental.pallas import tpu as pltpu
from jax.sharding import PartitionSpec as P

HEAD_DIM = 128
ROPE_BASE = 500000.0
NORM_EPS = 1e-5
MESH = pl.DeviceIdType.MESH
BF16, F32 = jnp.bfloat16, jnp.float32
VMEM_BYTES = 67043328
NIL, ONE, TWO, THREE, FOUR, EIGHT, SUB, LANES = 0, 1, 2, 3, 4, 8, 8, 128


def remote(src, dst, send_sem, recv_sem, to):
    return pltpu.make_async_remote_copy(src, dst, send_sem, recv_sem, device_id=to, device_id_type=MESH)


def start(copies):
    for c in copies:
        c.start()


def wait(copies):
    for c in copies:
        c.wait()


def top(n):
    return pl.ds(NIL, n)


def aligned(offset, n):
    return pl.ds(pl.multiple_of(offset, LANES), n)


def rope_tables(positions):
    half_dim = HEAD_DIM // 2
    inv_freq = jnp.power(jnp.float32(ROPE_BASE), -(jnp.arange(HEAD_DIM) % half_dim).astype(jnp.float32) * (2.0 / HEAD_DIM))
    angles = positions.astype(jnp.float32)[:, None] * inv_freq
    return jnp.cos(angles), jnp.sin(angles) * jnp.where(jnp.arange(HEAD_DIM) < half_dim, -1.0, 1.0)


def layer_kernel(chunks, cb, plan, x_hbm, seg, rope_c, rope_s, gain_a, gain_m, wq, wk, wv, wo, wg, wu, wd,
                 kc, vc, attn, wo_g, y_hbm,
                 wbuf, u2, hbuf, qb, seg_row, sgb, fq, fk, xmid, srow, sin, p_own, p_out, d_in, f_in, e_in, ystage,
                 xsem, wsem, sg_s, sg_r, k1s, k1r, k2s, k2r, kps, kpr, w1s, w1r, w2s, w2r, w3s, w3r, wps, wpr,
                 t_s, t_r, v_s, v_r, csem, lsem, osem, xrsem,
                 s_s, s_r, u1s, u1r, u2s, u2r, ups, upr, d_s, d_r, f_s, f_r, e_s, e_r, a_l, a_s, a_r, h_s, h_r):
    rows, dim = x_hbm.shape
    tp, sp = lax.axis_size("tp"), lax.axis_size("sp")
    hd = HEAD_DIM
    heads = wq.shape[ONE] // hd
    n_kv = wk.shape[ONE] // hd
    group = heads // n_kv
    wide = heads * hd
    col, wrow = dim // tp, wo.shape[NIL] // sp
    half = wrow // TWO
    nb = col // cb
    pair_w = TWO * cb
    ff = wg.shape[ONE] // TWO
    slots = wbuf.shape[NIL]
    per_dev = TWO * n_kv
    y, s = lax.axis_index("tp"), lax.axis_index("sp")
    core, chip, n_chip = s % TWO, s // TWO, sp // TWO
    yp, ym, y2 = (y + ONE) % tp, (y + tp - ONE) % tp, (y + TWO) % tp
    chip_at = lambda d: (chip + d) % n_chip * TWO
    up, dn, far = (chip_at(d) + core for d in (ONE, n_chip - ONE, TWO))
    pair = s + ONE - TWO * core
    to_pair, to_up, to_dn = ({"tp": y, "sp": d} for d in (pair, up, dn))
    to_p, to_m, to_2 = ({"tp": d, "sp": s} for d in (yp, ym, y2))
    scale2 = HEAD_DIM ** -0.5 * 1.4426950408889634

    kw = n_kv * hd
    n_x = xsem.shape[NIL]
    x_rows = rows // n_x
    x_copies = [pltpu.make_async_copy(x_hbm.at[pl.ds(i * x_rows, x_rows)], u2.at[pl.ds(i * x_rows, x_rows)], xsem.at[i])
                for i in range(n_x)]
    start(x_copies)
    kv_copies = [pltpu.make_async_copy(w, wbuf.at[NIL, :, pl.ds(i * kw, kw)], wsem.at[NIL, i]) for i, w in enumerate((wk, wv))]
    q_copies = [pltpu.make_async_copy(wq.at[:, pl.ds(t * TWO * kw, TWO * kw)], wbuf.at[ONE + t], wsem.at[ONE + t, NIL])
                for t in range(TWO)]

    barrier = pltpu.get_barrier_semaphore()
    for j in range(ONE, sp):
        pl.semaphore_signal(barrier, inc=ONE, device_id={"tp": y, "sp": (s + j) % sp}, device_id_type=MESH)
    for j in range(ONE, tp):
        pl.semaphore_signal(barrier, inc=ONE, device_id={"tp": (y + j) % tp, "sp": s}, device_id_type=MESH)

    def norm(i):
        x_copies[i].wait()
        step = x_rows // TWO

        @pl.loop(NIL, TWO)
        def _(j):
            rr = pl.ds(pl.multiple_of(i * x_rows + j * step, step), step)
            sq = jnp.zeros((step, LANES), F32)
            for b in range(dim // LANES):
                v = u2[rr, pl.ds(b * LANES, LANES)].astype(F32)
                sq += v * v
            inv = lax.rsqrt(jnp.sum(sq, axis=ONE, keepdims=True) * (1.0 / dim) + NORM_EPS)
            for b in range(dim // LANES):
                c = pl.ds(b * LANES, LANES)
                u2[rr, c] = (u2[rr, c].astype(F32) * inv * gain_a[:, c]).astype(BF16)

    seg_row[...] = jnp.broadcast_to(seg[...].astype(F32), (SUB, rows))
    norm(NIL)
    start(kv_copies)
    norm(ONE)
    pl.semaphore_wait(barrier, sp + tp - TWO)

    def w1(j):
        rank, mine = (y + j) % tp, aligned(s * wrow, wrow)
        return remote(wo.at[mine, aligned(rank * col, col)], wo_g.at[tp - ONE - j, mine],
                      w1s.at[j - ONE], w1r.at[tp - ONE - j], {"tp": rank, "sp": s})

    def sg(j):
        return remote(seg_row, sgb.at[s], sg_s.at[j], sg_r.at[j], {"tp": y, "sp": (s + j) % sp})

    for j in range(ONE, sp):
        sg(j).start()
    for j in range(ONE, tp):
        w1(j).start()

    def w_blk(i, dev, r0, n):
        return wo_g.at[i, pl.ds(pl.multiple_of(dev * wrow + r0, half), n)]

    def w2(i, side):
        b = w_blk(i, s, NIL, wrow)
        return remote(b, b, w2s.at[i, side], w2r.at[i, ONE - side], (to_up, to_dn)[side])

    def w3(i, side):
        b = w_blk(i, (up, dn)[side], (half, NIL)[side], half)
        return remote(b, b, w3s.at[i, side], w3r.at[i, side], (to_dn, to_up)[side])

    def wp(i, j):
        b = w_blk(i, (s, up, dn, far)[j], NIL, wrow)
        return remote(b, b, wps.at[i, j], wpr.at[i, j], to_pair)

    def w_start(i):
        w1(tp - ONE - i).wait_recv()
        w2(i, NIL).start()
        w2(i, ONE).start()
        wp(i, NIL).start()

    def w_mid(i):
        for side in range(TWO):
            w2(i, ONE - side).wait_recv()
            w3(i, side).start()
            wp(i, ONE + side).start()

    def w_last(i):
        w3(i, NIL).wait_recv()
        w3(i, ONE).wait_recv()
        wp(i, THREE).start()

    start(q_copies)
    for i in range(TWO, n_x):
        norm(i)

    def rope(t):
        return (t * rope_c[...] + pltpu.roll(t, hd // TWO, ONE) * rope_s[...]).astype(BF16)

    wait(kv_copies)
    r = jnp.dot(u2[top(rows), :], wbuf[NIL], preferred_element_type=F32)
    for g in range(n_kv):
        hbuf[s * per_dev + TWO * g] = rope(r[:, g * hd:(g + ONE) * hd])
        hbuf[s * per_dev + TWO * g + ONE] = r[:, kw + g * hd:kw + (g + ONE) * hd].astype(BF16)

    def k_blk(dev, g, lo=NIL, n=TWO):
        return hbuf.at[pl.ds(dev * per_dev + TWO * g + lo, n)]

    def k1(g, side):
        b = k_blk(s, g)
        return remote(b, b, k1s.at[g, side], k1r.at[g, ONE - side], (to_up, to_dn)[side])

    def k2(g, side):
        b = k_blk((up, dn)[side], g, ONE - side, ONE)
        return remote(b, b, k2s.at[g, side], k2r.at[g, side], (to_dn, to_up)[side])

    def kp(g, j):
        b = k_blk((s, up, dn, far)[j], g)
        return remote(b, b, kps.at[g, j], kpr.at[g, j], to_pair)

    def k_start(g):
        k1(g, NIL).start()
        k1(g, ONE).start()
        kp(g, NIL).start()

    def k_mid(g):
        for side in range(TWO):
            k1(g, ONE - side).wait_recv()
            k2(g, side).start()
            kp(g, ONE + side).start()

    def k_last(g):
        k2(g, NIL).wait_recv()
        k2(g, ONE).wait_recv()
        kp(g, THREE).start()

    k_start(NIL)

    for t in range(TWO):
        q_copies[t].wait()
        r = jnp.dot(u2[top(rows), :], wbuf[ONE + t], preferred_element_type=F32)
        for g in range(heads // TWO):
            qb[t * (heads // TWO) + g] = rope(r[:, g * hd:(g + ONE) * hd])

    n_o = -(-col // pair_w)
    part = wide
    starts = [sum(chunks[:i]) for i in range(len(chunks))]
    n_ch = len(chunks)

    def cols(block, width):
        return aligned(block * width, width)

    def o_width(t):
        return min(pair_w, col - t * pair_w)

    def o_part(t, j):
        w = o_width(t)
        src = wo_g.at[j - ONE, :, pl.ds(t * pair_w, w)] if j else wo.at[:, aligned(y * col + t * pair_w, w)]
        return pltpu.make_async_copy(src, wbuf.at[t, aligned((y + j) % tp * part, part), top(w)], osem.at[t, j])

    def rows_of(i, row0, n):
        return pl.ds(TWO * starts[i] + row0, n)

    xr_copies = [pltpu.make_async_copy(x_hbm.at[pl.ds(r0, r), cols(y, col)], u2.at[rows_of(i, NIL, r), cols(y, col)], xrsem.at[i])
                 for i, (r0, r) in enumerate(zip(starts, chunks))]
    start(xr_copies)
    for t in range(n_o):
        o_part(t, NIL).start()

    for j in range(ONE, sp):
        sg(j).wait_recv()
    sgb[s] = seg_row[...]
    lane = lax.broadcasted_iota(jnp.int32, (rows, LANES), ONE).astype(F32)

    def seg_col(dev):
        return jnp.broadcast_to(sgb[dev, top(ONE), :], (LANES, rows)).T

    fq[...] = jnp.where(seg_col(s) == lane, 1.0, 0.0).astype(BF16)

    @pl.loop(NIL, sp)
    def _(b):
        fk[b] = jnp.where(seg_col(b) == lane, 0.0, -1e30).astype(BF16)

    def attend(h, i, g, b0, nb, own):
        nk = nb * rows
        both = lambda j: jnp.concatenate([hbuf[(b0 + d) * per_dev + TWO * g + j] for d in range(nb)], axis=NIL)
        q = jnp.concatenate([qb[h], fq[...]], axis=ONE)
        k = jnp.concatenate([both(NIL), fk[pl.ds(b0, nb)].reshape(nk, LANES)], axis=ONE)
        v = both(ONE)
        sc = lax.dot_general(q, k, (((ONE,), (ONE,)), ((), ())), preferred_element_type=F32)
        if own:
            lo = nk - rows
            a, b = (lax.broadcasted_iota(jnp.int32, (rows, rows), d) for d in range(TWO))
            tail = jnp.where(a >= b, sc[:, lo:], -1e30)
            sc = jnp.concatenate([sc[:, :lo], tail], axis=ONE) if lo else tail
        at = aligned(i * rows, rows)
        mx = jnp.max(sc, axis=ONE, keepdims=True)
        if own:
            mn = jnp.broadcast_to(mx, (rows, LANES))
        else:
            mn = jnp.maximum(xmid[group + i], mx)
            al = jnp.exp2((xmid[group + i] - mn) * scale2)
        ps = [jnp.exp2((sc[:, j * LANES:(j + ONE) * LANES] - mn) * scale2) for j in range(nk // LANES)]
        ls = functools.reduce(jnp.add, ps)
        o = jnp.dot(jnp.concatenate([p.astype(BF16) for p in ps], axis=ONE), v, preferred_element_type=F32)
        xmid[group + i] = mn
        if own:
            p_own[at, top(LANES)] = ls
            xmid[i] = o
        else:
            p_own[at, top(LANES)] = p_own[at, top(LANES)] * al + ls
            xmid[i] = xmid[i] * al + o

    def a_at(rank, h, r0, n):
        return attn.at[pl.ds(r0, n), aligned(rank * wide + h * hd, hd)]

    def a1(h, side):
        return remote(qb.at[h], a_at(y, h, NIL, rows), t_s.at[side, h], t_r.at[ONE - side, h], (to_p, to_m)[side])

    def a2(h, side):
        b = a_at((yp, ym)[side], h, (rows // TWO, NIL)[side], rows // TWO)
        return remote(b, b, v_s.at[side, h], v_r.at[side, h], (to_m, to_p)[side])

    def pass_on(h):
        for side in range(TWO):
            a1(h, ONE - side).wait_recv()
            a2(h, side).start()

    @pl.loop(NIL, n_kv)
    def _(g):
        @pl.when(g == NIL)
        def _():
            k_mid(NIL)
            k_start(ONE)

        kp(g, NIL).wait_recv()

        @pl.loop(NIL, group)
        def _(i):
            @pl.when(core == NIL)
            def _():
                attend(g * group + i, i, g, s, ONE, True)

            @pl.when(core == ONE)
            def _():
                attend(g * group + i, i, g, chip_at(NIL), TWO, True)

        k_last(g)
        for j in range(ONE, FOUR):
            kp(g, j).wait_recv()

        @pl.loop(NIL, group)
        def _(i):
            h = g * group + i

            @pl.when(chip >= ONE)
            def _():
                attend(h, i, g, chip_at(n_chip - ONE), TWO, False)

            @pl.when(chip == n_chip - ONE)
            def _():
                attend(h, i, g, chip_at(ONE), TWO, False)

            @pl.when(chip >= TWO)
            def _():
                attend(h, i, g, chip_at(TWO), TWO, False)

            total = jnp.sum(p_own[aligned(i * rows, rows), top(LANES)], axis=ONE, keepdims=True)
            qb[h] = (xmid[i] / total).astype(BF16)
            a1(h, NIL).start()
            a1(h, ONE).start()

            @pl.when(h == NIL)
            def _():
                k_mid(ONE)
                for b in range(tp - ONE):
                    w_start(b)

            for b in range(tp - TWO):
                @pl.when(h == heads - FOUR + b)
                def _():
                    w_mid(b)

            @pl.when(h >= TWO)
            def _():
                pass_on(h - TWO)

    mine_kv = s // (sp // n_kv)
    caches = [pltpu.make_async_copy(hbuf.at[d * per_dev + TWO * mine_kv + i], c.at[pl.ds(d * rows, rows)], csem.at[i, d])
              for i, c in enumerate((kc, vc)) for d in range(sp)]
    start(caches)
    pass_on(heads - TWO)
    w_mid(tp - TWO)
    pass_on(heads - ONE)

    def w_done(i):
        for j in range(FOUR):
            wp(i, j).wait_recv()
        for t in range(n_o):
            o_part(t, i + ONE).start()

    for g in range(n_kv):
        for j in range(FOUR):
            kp(g, j).wait_send()
        for side in range(TWO):
            k1(g, side).wait_send()
            k2(g, side).wait_send()
    wait(caches)

    def head_in(d, h):
        rank = (y + d) % tp
        return pltpu.make_async_copy(a_at(rank, h, NIL, rows), hbuf.at[rank * heads + h], lsem.at[d, h])

    for h in range(heads):
        hbuf[y * heads + h] = qb[h]
        head_in(ONE, h).start()
        head_in(THREE, h).start()

    for i in range(tp - ONE):
        w_last(i)
        if i:
            w_done(i - ONE)
    for h in range(heads):
        for side in range(TWO):
            a2(h, side).wait_recv()
        head_in(TWO, h).start()
    w_done(tp - TWO)
    for h in range(heads):
        for d in range(ONE, tp):
            head_in(d, h).wait()

    def wide_rows(r0, n):
        return jnp.concatenate([hbuf[b, pl.ds(r0, n)] for b in range(hbuf.shape[NIL])], axis=ONE)

    def front_sent():
        @pl.loop(NIL, heads)
        def _(h):
            for side in range(TWO):
                a1(h, side).wait_send()
                a2(h, side).wait_send()
        for i in range(tp - ONE):
            w1(i + ONE).wait_send()
            for j in range(FOUR):
                wp(i, j).wait_send()
            for side in range(TWO):
                w2(i, side).wait_send()
                w3(i, side).wait_send()
        for j in range(ONE, sp):
            sg(j).wait_send()

    n_g, n_d = ff // pair_w, nb * tp // FOUR

    def g_tile(n, slot, which):
        c = aligned(core * ff + n * pair_w, pair_w)
        return pltpu.make_async_copy((wg, wu)[which].at[:, c], wbuf.at[slot], wsem.at[slot, NIL])

    def g_pair(n, base):
        return [g_tile(n, (base + TWO * n + i) % slots, i) for i in range(TWO)]

    def d_cols(m):
        q = m // nb
        d = (TWO + THREE * q + THREE * (q * (q - ONE) // TWO)) % FOUR
        return aligned((y + d) % tp * col + m % nb * cb, cb)

    def d_tile(p, slot):
        return [pltpu.make_async_copy(wd.at[aligned(core * ff, ff), d_cols(TWO * p + i)],
                                      wbuf.at[slot, top(ff), pl.ds(i * cb, cb)], wsem.at[slot, i]) for i in range(TWO)]

    def d_pair(p, base):
        return [c for i in range(TWO) for c in d_tile(TWO * p + i, (base + TWO * p + i) % slots)]

    base = n_o

    lanes = srow.shape[-ONE]

    def stat(i, j):
        return remote(srow.at[i], sin.at[i, j], s_s.at[i, j], s_r.at[i, j], (to_p, to_m, to_2)[j])

    def x1_rows(i):
        r0, r = starts[i], chunks[i]
        for t in range(n_o):
            w = o_width(t)
            if not i:
                wait([o_part(t, j) for j in range(tp)])
            v = jnp.dot(wide_rows(r0, r), wbuf[t, top(tp * part), top(w)], preferred_element_type=F32)
            for q in range(w // LANES):
                xmid[t * FOUR + q, pl.ds(r0, r)] = v[:, q * LANES:(q + ONE) * LANES]
        sq = jnp.zeros((r, LANES), F32)
        for b in range(col // LANES):
            v = xmid[b, pl.ds(r0, r)] + u2[rows_of(i, NIL, r), aligned(y * col + b * LANES, LANES)].astype(F32)
            xmid[b, pl.ds(r0, r)] = v
            sq += v * v
        tot = jnp.broadcast_to(jnp.sum(sq, axis=ONE, keepdims=True), (r, LANES))
        if r < lanes:
            tot = jnp.concatenate([tot, jnp.zeros((lanes - r, LANES), F32)], axis=NIL)
        srow[i] = tot.T[:SUB, :]
        for j in range(tp - ONE):
            stat(i, j).start()

    def norm_rows(i):
        r0, r = starts[i], chunks[i]
        for j in range(tp - ONE):
            stat(i, j).wait()
        tot = srow[i]
        for j in range(tp - ONE):
            tot += sin[i, j]
        inv = lax.rsqrt(tot * (1.0 / dim) + NORM_EPS)
        inv = jnp.broadcast_to(inv[:ONE, :], (LANES, lanes)).T[:r, :]
        for b in range(col // LANES):
            c = aligned(y * col + b * LANES, LANES)
            u2[rows_of(i, NIL, r), c] = (xmid[b, pl.ds(r0, r)] * inv * gain_m[:, c]).astype(BF16)

    def u_blk(i, row0, n_rows, rank):
        return u2.at[rows_of(i, row0, n_rows), cols(rank, col)]

    def u_first(i, side, turn):
        h = chunks[i] // TWO
        b = u_blk(i, h * (side + turn - TWO * side * turn), h, y)
        return remote(b, b, u1s.at[i, side, turn], u1r.at[i, ONE - side, turn], (to_p, to_m)[side])

    def u_second(i, side):
        h = chunks[i] // TWO
        b = u_blk(i, h, h, yp) if side == NIL else u_blk(i, NIL, h, ym)
        return remote(b, b, u2s.at[i, side], u2r.at[i, side], (to_m, to_p)[side])

    def u_pair(i, j):
        r, rank = chunks[i], (y, yp, ym, y2)[j]
        return remote(u_blk(i, NIL, r, rank), u_blk(i, r, r, rank), ups.at[i, j], upr.at[i, j], to_pair)

    def u_start(i):
        for turn in range(TWO):
            u_first(i, NIL, turn).start()
            u_first(i, ONE, turn).start()
        u_pair(i, NIL).start()

    def u_mid(i):
        for side in range(TWO):
            u_first(i, ONE - side, NIL).wait_recv()
            u_second(i, side).start()

    def u_last(i):
        for side in range(TWO):
            u_first(i, ONE - side, ONE).wait_recv()
            u_pair(i, ONE + side).start()
        for side in range(TWO):
            u_second(i, side).wait_recv()
        u_pair(i, THREE).start()

    def u_ready(i):
        for j in range(FOUR):
            u_pair(i, j).wait_recv()

    def u_drain(i):
        for side in range(TWO):
            for turn in range(TWO):
                u_first(i, side, turn).wait_send()
            u_second(i, side).wait_send()
        for j in range(FOUR):
            u_pair(i, j).wait_send()

    def blk_rows(m, row0, n):
        return pl.ds(pl.multiple_of(m * max(chunks) + row0, EIGHT), n)

    def d_copy(i, m, slot):
        r, par = chunks[i], i % TWO
        return remote(p_out.at[slot, top(r)], d_in.at[par, m, top(r)], d_s.at[slot], d_r.at[par, m], to_pair)

    def t_add(i, m):
        r, par = chunks[i], i % TWO
        d_copy(i, m, NIL).wait_recv()
        p_own[blk_rows(m, NIL, r), :] += d_in[par, m, top(r)]

    def f_copy(i, k, side):
        h, par = chunks[i] // TWO, i % TWO
        return remote(p_own.at[blk_rows(k, side * h, h)], f_in.at[par, side, k, top(h)],
                      f_s.at[side, k], f_r.at[par, side, k], (to_m, to_p)[side])

    def t_f(i, k):
        f_copy(i, k, NIL).start()
        f_copy(i, k, ONE).start()

    def e_copy(i, k, side):
        r, par = chunks[i], i % TWO
        return remote(p_own.at[blk_rows((TWO - side) * nb + k, NIL, r)], e_in.at[par, side, k, top(r)],
                      e_s.at[side, k], e_r.at[par, side, k], (to_m, to_p)[side])

    def t_e(i, k, side):
        h, par = chunks[i] // TWO, i % TWO
        f_copy(i, k, side).wait_recv()
        p_own[blk_rows((TWO - side) * nb + k, side * h, h), :] += f_in[par, side, k, top(h)]
        e_copy(i, k, side).start()

    def y_at(i, row0, n_rows, rank, k):
        return y_hbm.at[pl.ds(starts[i] + row0, n_rows), aligned(rank * col + k * cb, cb)]

    def a_copy_y(i, k, side):
        r, par = chunks[i], i % TWO
        return remote(ystage.at[par, k, top(r)], y_at(i, NIL, r, y, k), a_s.at[par, side, k], a_r.at[par, ONE - side, k],
                      (to_p, to_m)[side])

    def a_local(i, k):
        r, par = chunks[i], i % TWO
        return pltpu.make_async_copy(ystage.at[par, k, top(r)], y_at(i, NIL, r, y, k), a_l.at[par, k])

    def h_copy(i, k, side):
        h = chunks[i] // TWO
        b = y_at(i, h, h, yp, k) if side == NIL else y_at(i, NIL, h, ym, k)
        return remote(b, b, h_s.at[i, side, k], h_r.at[i, side, k], (to_m, to_p)[side])

    def t_final(i, k):
        r, par = chunks[i], i % TWO
        for side in range(TWO):
            e_copy(i, k, side).wait_recv()
        v = (p_own[blk_rows(THREE * nb + k, NIL, r), :] + e_in[par, NIL, k, top(r)] + e_in[par, ONE, k, top(r)]
             + jnp.concatenate([xmid[TWO * k + q, pl.ds(starts[i], r)] for q in range(TWO)], axis=ONE))
        ystage[par, k, top(r)] = v.astype(BF16)
        for side in range(TWO):
            a_copy_y(i, k, side).start()
        a_local(i, k).start()

    def t_fwd(i, k):
        for side in range(TWO):
            a_copy_y(i, k, ONE - side).wait_recv()
            h_copy(i, k, side).start()

    def sums_sent(i):
        for k in range(nb):
            for side in range(TWO):
                f_copy(i, k, side).wait_send()
                e_copy(i, k, side).wait_send()

    def rows_done(i):
        for k in range(nb):
            for side in range(TWO):
                h_copy(i, k, side).wait_recv()
                h_copy(i, k, side).wait_send()
                a_copy_y(i, k, side).wait_send()
            a_local(i, k).wait()

    g_tile(NIL, base, NIL).start()
    wait(xr_copies)
    for i in range(n_ch):
        x1_rows(i)
        if i == ONE:
            norm_rows(NIL)
            u_start(NIL)
    g_tile(NIL, NIL, ONE).start()
    norm_rows(ONE)
    u_mid(NIL)
    u_start(ONE)
    front_sent()
    for i in range(TWO, n_ch):
        norm_rows(i)
    u_last(NIL)
    u_ready(NIL)

    tasks = {"mid": u_mid, "last": u_last, "start": u_start, "e": t_e, "final": t_final, "fwd": t_fwd}

    def run(todo, at):
        for when, name, *args in todo:
            @pl.when(at == when)
            def _():
                tasks[name](*args)

    for i in range(n_ch):
        r = chunks[i]
        g_base, d_base = base % slots, (base + TWO * n_g) % slots
        base += TWO * (n_g + n_d)

        @pl.loop(NIL, n_g)
        def _(j):
            @pl.when(j + ONE < n_g)
            def _():
                start(g_pair(j + ONE, g_base))

            @pl.when(j + ONE >= n_g)
            def _():
                start(d_pair(NIL, d_base))

            wait(g_pair(j, g_base))
            g, u = (jnp.dot(u2[rows_of(i, NIL, TWO * r), :], wbuf[(g_base + TWO * j + q) % slots], preferred_element_type=F32)
                    for q in range(TWO))
            g = (jax.nn.silu(g) * u).astype(BF16)
            for q in range(FOUR):
                hbuf[FOUR * j + q, top(TWO * r)] = g[:, q * LANES:(q + ONE) * LANES]
            run(plan[i][NIL], j)

        if i:
            sums_sent(i - ONE)

        @pl.loop(NIL, n_d)
        def _(p):
            @pl.when(p + ONE < n_d)
            def _():
                start(d_pair(p + ONE, d_base))

            if i + ONE < n_ch:
                @pl.when(p + ONE >= n_d)
                def _():
                    start(g_pair(NIL, base % slots))

            wait(d_pair(p, d_base))
            out = p % TWO * FOUR

            @pl.when(p >= TWO)
            def _():
                for q in range(FOUR):
                    d_copy(i, q, out + q).wait_send()

            for q in range(TWO):
                v = jnp.dot(wide_rows(NIL, TWO * r), wbuf[(d_base + TWO * p + q) % slots, top(ff)],
                            preferred_element_type=F32)
                for e in range(TWO):
                    b = TWO * q + e
                    p_own[blk_rows(FOUR * p + b, NIL, r), :] = v[:r, e * cb:(e + ONE) * cb]
                    p_out[out + b, top(r)] = v[r:, e * cb:(e + ONE) * cb]
            for q in range(FOUR):
                d_copy(i, FOUR * p + q, out + q).start()

            @pl.when(p >= ONE)
            def _():
                for q in range(FOUR):
                    t_add(i, FOUR * (p - ONE) + q)

            @pl.when(p == ONE)
            def _():
                for k in range(FOUR):
                    t_f(i, k)

            @pl.when(p == TWO)
            def _():
                for k in range(FOUR, nb):
                    t_f(i, k)
            run(plan[i][ONE], p)

        for q in range(FOUR):
            t_add(i, FOUR * (n_d - ONE) + q)
        for q in range(FOUR):
            for out in range(TWO):
                d_copy(i, q, FOUR * out + q).wait_send()
        for name, *args in plan[i][TWO]:
            tasks[name](*args)
        if i + ONE < n_ch:
            u_ready(i + ONE)

    last = n_ch - ONE
    if last >= TWO:
        rows_done(last - TWO)
    for k in range(nb):
        t_final(last, k)
        if k >= TWO:
            t_fwd(last, k - TWO)
    for k in range(nb - TWO, nb):
        t_fwd(last, k)
    for i in range(max(last - ONE, NIL), n_ch):
        rows_done(i)
    sums_sent(last)
    for i in range(n_ch):
        u_drain(i)


CHUNKS = (192, 192, 128)


def mlp_plan():
    early = lambda i: [(3, "e", i, 0, 1), (3, "e", i, 1, 1), (4, "e", i, 2, 1), (4, "e", i, 0, 0), (4, "e", i, 1, 0)]
    late = lambda i: [("e", i, 3, 1), ("e", i, 2, 0), ("e", i, 4, 1), ("e", i, 3, 0), ("e", i, 4, 0)]
    at_start = lambda i: [(0, *t) for t in late(i)]
    finals = lambda i, at: [(a, "final", i, k) for k, a in enumerate(at)]
    passed = lambda i, at: [(a, "fwd", i, k) for k, a in enumerate(at)]
    gather = [(1, "mid", 1), (1, "start", 2), (3, "last", 1), (4, "mid", 2), (6, "last", 2)]
    return ((gather, early(0), ()),
            (at_start(0) + finals(0, (1, 2, 3, 4, 5)) + passed(0, (5, 6, 6, 6, 7)), early(1), ()),
            (at_start(1) + finals(1, (2, 3, 4, 6, 7)), passed(1, (0, 1, 1, 2, 2)) + early(2), late(2)))


def layer_call(x_in, positions, segments, gain_a, gain_m, wq, wk, wv, wo, wg, wu, wd):
    rows, dim = x_in.shape
    tp, sp = lax.axis_size("tp"), lax.axis_size("sp")
    heads, n_kv = wq.shape[ONE] // HEAD_DIM, wk.shape[ONE] // HEAD_DIM
    cb = TWO * LANES
    col, ff = dim // tp, wg.shape[ONE] // TWO
    nb = col // cb
    n_ch, rm = len(CHUNKS), max(CHUNKS)
    lanes = -(-rm // LANES) * LANES
    rope_c, rope_s = rope_tables(positions)
    dma = pltpu.SemaphoreType.DMA
    hbm, vmem = pl.BlockSpec(memory_space=pl.ANY), pl.BlockSpec(memory_space=pltpu.VMEM)
    bufs = [((FOUR, dim, TWO * cb), BF16), ((TWO * rows, dim), BF16), ((ff // LANES, rows, LANES), BF16),
            ((heads, rows, HEAD_DIM), BF16), ((SUB, rows), F32), ((sp, SUB, rows), F32), ((rows, LANES), BF16),
            ((sp, rows, LANES), BF16), ((col // LANES, rows, LANES), F32), ((n_ch, SUB, lanes), F32), ((n_ch, tp - ONE, SUB, lanes), F32),
            ((tp * nb * rm, cb), F32), ((EIGHT, rm, cb), F32), ((TWO, tp * nb, rm, cb), F32),
            ((TWO, TWO, nb, rm // TWO, cb), F32), ((TWO, TWO, nb, rm, cb), F32), ((TWO, nb, rm, cb), BF16)]
    sems = [(FOUR,), (FOUR, TWO), (sp,), (sp,)] + [(n_kv, TWO)] * FOUR + [(n_kv, FOUR)] * TWO + [(tp - ONE,)] * TWO
    sems += [(tp - ONE, TWO)] * FOUR + [(tp - ONE, FOUR)] * TWO + [(TWO, heads)] * FOUR + [(TWO, sp), (tp, heads), (THREE, tp), (n_ch,)]
    sems += [(n_ch, tp - ONE)] * TWO + [(n_ch, TWO, TWO)] * TWO + [(n_ch, TWO)] * TWO + [(n_ch, FOUR)] * TWO
    sems += [(EIGHT,), (TWO, tp * nb)] + [(TWO, nb), (TWO, TWO, nb)] * TWO + [(TWO, nb)] + [(TWO, TWO, nb)] * TWO
    sems += [(n_ch, TWO, nb)] * TWO
    cache = jax.ShapeDtypeStruct((sp * rows, HEAD_DIM), BF16)
    kc, vc, _, _, y_out = pl.pallas_call(
        functools.partial(layer_kernel, CHUNKS, cb, mlp_plan()), name="layer",
        out_shape=[cache, cache, jax.ShapeDtypeStruct((rows, tp * heads * HEAD_DIM), BF16), jax.ShapeDtypeStruct((tp - ONE, wo.shape[NIL], col), BF16),
                   jax.ShapeDtypeStruct((rows, dim), BF16)],
        in_specs=[hbm] + [vmem] * (FOUR + ONE) + [hbm] * (FOUR + THREE), out_specs=[hbm] * (FOUR + ONE),
        scratch_shapes=[pltpu.VMEM(*b) for b in bufs] + [dma(q) for q in sems],
        compiler_params=pltpu.CompilerParams(collective_id=ONE, has_side_effects=True, vmem_limit_bytes=VMEM_BYTES),
    )(x_in, segments.reshape(ONE, rows), rope_c, rope_s, gain_a.reshape(ONE, dim), gain_m.reshape(ONE, dim),
      wq, wk, wv, wo, wg, wu, wd)
    return y_out, kc, vc


def solution(mesh):
    row_spec = P(("rep", "sp"), None)
    tok_spec = P(("rep", "sp"))
    full_spec = P(None)
    col_spec = P(None, "tp")
    wrow_spec = P("tp", None)
    cache_spec = P("rep", ("tp", "sp"), None)

    def local_layer(x_in, positions, segments, gain_attn, w_q, w_k, w_v, w_o, gain_mlp, w_gate, w_up, w_down):
        y_out, kc, vc = layer_call(x_in, positions, segments, gain_attn, gain_mlp, w_q, w_k, w_v, w_o, w_gate, w_up, w_down)
        return y_out, kc.reshape(-1, 1, HEAD_DIM), vc.reshape(-1, 1, HEAD_DIM)

    return jax.shard_map(local_layer, mesh=mesh,
                         in_specs=(row_spec, tok_spec, tok_spec, full_spec, col_spec, col_spec, col_spec, wrow_spec,
                                   full_spec, col_spec, col_spec, wrow_spec),
                         out_specs=(row_spec, cache_spec, cache_spec), check_vma=False)
```

time: 316 us -> 305 us (0.965)
  the two profiles are of different devices: /device:TPU:97 before, /device:TPU:102 now
where the time goes in v3:
time: 305 us; the launch traced here: 299 us
  Pallas kernels  288 us (94%)
  local copies, waits for them, and re-layouts  7.28 us (2%)
    pallas_call x1, Pallas kernels, layer_call(): pl.pallas_call(functools.partial(layer_kernel, CHUNKS, cb, mlp_plan()), n...  288 us
    unnamed x7, local copies, waits for them, and re-layouts  7.28 us

profile of v3, /device:TPU:102, one launch (start us, length us, event | category | flops | bytes accessed | tf_op | source)
XLA Modules:
  0.0 299.3 jit_solution(15724537638330668291)
XLA Ops:
  0.6 0.7 convert_element_type.10
  1.3 1.8 fusion
  3.1 288.4 %layer.1 = (bf16[4096,128]{1,0:T(8,128)(2,1)}, bf16[4096,128]{1,0:T(8,128)(2,1)}, bf16[512,4096]{1,0:T(8,128)(2,1)}, bf16[3,1024,1280]{2,1,0:T(8,128)(2,1)}, bf16[512,5120]{1,0:T(8,128)(2,1)}) custom-call(bf16[512,5120]{1,0:T(8,128)(2,1)} %x_hbm.1, s32[1,512]{1,0:T(1,128)} %bitcast.9, f32[512,128]{1,0:T(8,128)} %get-tuple-element.10.rope_c, ...), custom_call_target="tpu_custom_call" | custom-call | tf_op jit(solution)/shard_map/layer/pallas_call | solution.py:768
  291.6 0.0 copy-start.1
  291.6 0.0 copy-start
  291.6 5.3 %copy.18 = bf16[512,5120]{1,0:T(8,128)(2,1)} copy(bf16[512,5120]{1,0:T(8,128)(2,1)} %get-tuple-element.16) | data formatting | bytes 10485760
  296.9 0.0 copy-done.1
  296.9 1.0 copy.19
  297.9 0.0 copy-done
  297.9 1.0 copy.20
  (1 shorter events, 0.0 us)
Async XLA Ops:
  291.6 5.4 %copy-start.1 = (bf16[4096,128]{1,0:T(8,128)(2,1)S(1)}, bf16[4096,128]{1,0:T(8,128)(2,1)}, u32[]{:S(2)}) copy-start(bf16[4096,128]{1,0:T(8,128)(2,1)} %get-tuple-element.7) | copy-start | bytes 3145732
  291.6 6.3 %copy-start = (bf16[4096,128]{1,0:T(8,128)(2,1)S(1)}, bf16[4096,128]{1,0:T(8,128)(2,1)}, u32[]{:S(2)}) copy-start(bf16[4096,128]{1,0:T(8,128)(2,1)} %get-tuple-element.8) | copy-start | bytes 3145732

commit v4 on v3

--- a/solution.py
+++ b/solution.py
@@ -2,6 +2,7 @@
 
 import jax
 import jax.numpy as jnp
+import numpy as np
 from jax import lax
 from jax.experimental import pallas as pl
 from jax.experimental.pallas import tpu as pltpu
@@ -38,16 +39,9 @@
     return pl.ds(pl.multiple_of(offset, LANES), n)
 
 
-def rope_tables(positions):
-    half_dim = HEAD_DIM // 2
-    inv_freq = jnp.power(jnp.float32(ROPE_BASE), -(jnp.arange(HEAD_DIM) % half_dim).astype(jnp.float32) * (2.0 / HEAD_DIM))
-    angles = positions.astype(jnp.float32)[:, None] * inv_freq
-    return jnp.cos(angles), jnp.sin(angles) * jnp.where(jnp.arange(HEAD_DIM) < half_dim, -1.0, 1.0)
-
-
-def layer_kernel(chunks, cb, plan, x_hbm, seg, rope_c, rope_s, gain_a, gain_m, wq, wk, wv, wo, wg, wu, wd,
+def layer_kernel(chunks, cb, plan, x_hbm, seg, pos, freq, gain_a, gain_m, wq, wk, wv, wo, wg, wu, wd,
                  kc, vc, attn, wo_g, y_hbm,
-                 wbuf, u2, hbuf, qb, seg_row, sgb, fq, fk, xmid, srow, sin, p_own, p_out, d_in, f_in, e_in, ystage,
+                 wbuf, u2, hbuf, qb, rope_c, rope_s, seg_row, sgb, fq, xmid, srow, sin, p_own, p_out, d_in, f_in, e_in, ystage,
                  xsem, wsem, sg_s, sg_r, k1s, k1r, k2s, k2r, kps, kpr, w1s, w1r, w2s, w2r, w3s, w3r, wps, wpr,
                  t_s, t_r, v_s, v_r, csem, lsem, osem, xrsem,
                  s_s, s_r, u1s, u1r, u2s, u2r, ups, upr, d_s, d_r, f_s, f_r, e_s, e_r, a_l, a_s, a_r, h_s, h_r):
@@ -82,8 +76,9 @@
                 for i in range(n_x)]
     start(x_copies)
     kv_copies = [pltpu.make_async_copy(w, wbuf.at[NIL, :, pl.ds(i * kw, kw)], wsem.at[NIL, i]) for i, w in enumerate((wk, wv))]
-    q_copies = [pltpu.make_async_copy(wq.at[:, pl.ds(t * TWO * kw, TWO * kw)], wbuf.at[ONE + t], wsem.at[ONE + t, NIL])
-                for t in range(TWO)]
+
+    def q_copy(t):
+        return pltpu.make_async_copy(wq.at[:, aligned(t * TWO * kw, TWO * kw)], wbuf.at[ONE + t], wsem.at[ONE + t, NIL])
 
     barrier = pltpu.get_barrier_semaphore()
     for j in range(ONE, sp):
@@ -158,7 +153,8 @@
         w3(i, ONE).wait_recv()
         wp(i, THREE).start()
 
-    start(q_copies)
+    q_copy(NIL).start()
+    q_copy(ONE).start()
     for i in range(TWO, n_x):
         norm(i)
 
@@ -166,6 +162,10 @@
         return (t * rope_c[...] + pltpu.roll(t, hd // TWO, ONE) * rope_s[...]).astype(BF16)
 
     wait(kv_copies)
+    angles = jnp.broadcast_to(pos[...].astype(F32), (LANES, rows)).T * freq[...]
+    sign = jnp.where(lax.broadcasted_iota(jnp.int32, (rows, hd), ONE) < hd // TWO, -1.0, 1.0)
+    rope_c[...] = jnp.cos(angles)
+    rope_s[...] = jnp.sin(angles) * sign
     r = jnp.dot(u2[top(rows), :], wbuf[NIL], preferred_element_type=F32)
     for g in range(n_kv):
         hbuf[s * per_dev + TWO * g] = rope(r[:, g * hd:(g + ONE) * hd])
@@ -204,8 +204,9 @@
 
     k_start(NIL)
 
-    for t in range(TWO):
-        q_copies[t].wait()
+    @pl.loop(NIL, TWO)
+    def _(t):
+        q_copy(t).wait()
         r = jnp.dot(u2[top(rows), :], wbuf[ONE + t], preferred_element_type=F32)
         for g in range(heads // TWO):
             qb[t * (heads // TWO) + g] = rope(r[:, g * hd:(g + ONE) * hd])
@@ -243,17 +244,21 @@
     def seg_col(dev):
         return jnp.broadcast_to(sgb[dev, top(ONE), :], (LANES, rows)).T
 
+    def key_cols(b):
+        return aligned(yp * col + b * LANES, LANES)
+
     fq[...] = jnp.where(seg_col(s) == lane, 1.0, 0.0).astype(BF16)
 
     @pl.loop(NIL, sp)
     def _(b):
-        fk[b] = jnp.where(seg_col(b) == lane, 0.0, -1e30).astype(BF16)
+        u2[pl.ds(rows, rows), key_cols(b)] = jnp.where(seg_col(b) == lane, 0.0, -1e30).astype(BF16)
 
     def attend(h, i, g, b0, nb, own):
         nk = nb * rows
         both = lambda j: jnp.concatenate([hbuf[(b0 + d) * per_dev + TWO * g + j] for d in range(nb)], axis=NIL)
         q = jnp.concatenate([qb[h], fq[...]], axis=ONE)
-        k = jnp.concatenate([both(NIL), fk[pl.ds(b0, nb)].reshape(nk, LANES)], axis=ONE)
+        feat = jnp.concatenate([u2[pl.ds(rows, rows), key_cols(b0 + d)] for d in range(nb)], axis=NIL)
+        k = jnp.concatenate([both(NIL), feat], axis=ONE)
         v = both(ONE)
         sc = lax.dot_general(q, k, (((ONE,), (ONE,)), ((), ())), preferred_element_type=F32)
         if own:
@@ -321,17 +326,11 @@
         def _(i):
             h = g * group + i
 
-            @pl.when(chip >= ONE)
-            def _():
-                attend(h, i, g, chip_at(n_chip - ONE), TWO, False)
-
-            @pl.when(chip == n_chip - ONE)
-            def _():
-                attend(h, i, g, chip_at(ONE), TWO, False)
-
-            @pl.when(chip >= TWO)
-            def _():
-                attend(h, i, g, chip_at(TWO), TWO, False)
+            @pl.loop(ONE, n_chip)
+            def _(e):
+                @pl.when(chip >= e)
+                def _():
+                    attend(h, i, g, chip_at(n_chip - e), TWO, False)
 
             total = jnp.sum(p_own[aligned(i * rows, rows), top(LANES)], axis=ONE, keepdims=True)
             qb[h] = (xmid[i] / total).astype(BF16)
@@ -446,13 +445,21 @@
 
     def x1_rows(i):
         r0, r = starts[i], chunks[i]
-        for t in range(n_o):
-            w = o_width(t)
-            if not i:
-                wait([o_part(t, j) for j in range(tp)])
+        def tile(t, w):
             v = jnp.dot(wide_rows(r0, r), wbuf[t, top(tp * part), top(w)], preferred_element_type=F32)
             for q in range(w // LANES):
                 xmid[t * FOUR + q, pl.ds(r0, r)] = v[:, q * LANES:(q + ONE) * LANES]
+
+        if not i:
+            for t in range(n_o):
+                wait([o_part(t, j) for j in range(tp)])
+
+        @pl.loop(NIL, col // pair_w)
+        def _(t):
+            tile(t, pair_w)
+
+        if col % pair_w:
+            tile(n_o - ONE, col % pair_w)
         sq = jnp.zeros((r, LANES), F32)
         for b in range(col // LANES):
             v = xmid[b, pl.ds(r0, r)] + u2[rows_of(i, NIL, r), aligned(y * col + b * LANES, LANES)].astype(F32)
@@ -506,13 +513,19 @@
             u_first(i, ONE - side, NIL).wait_recv()
             u_second(i, side).start()
 
-    def u_last(i):
+    def u_near(i):
         for side in range(TWO):
             u_first(i, ONE - side, ONE).wait_recv()
             u_pair(i, ONE + side).start()
+
+    def u_far(i):
         for side in range(TWO):
             u_second(i, side).wait_recv()
         u_pair(i, THREE).start()
+
+    def u_last(i):
+        u_near(i)
+        u_far(i)
 
     def u_ready(i):
         for j in range(FOUR):
@@ -607,22 +620,55 @@
 
     g_tile(NIL, base, NIL).start()
     wait(xr_copies)
-    for i in range(n_ch):
+    x1_rows(NIL)
+    x1_rows(n_ch - ONE)
+    norm_rows(NIL)
+    u_start(NIL)
+    for i in range(ONE, n_ch - ONE):
         x1_rows(i)
-        if i == ONE:
-            norm_rows(NIL)
-            u_start(NIL)
     g_tile(NIL, NIL, ONE).start()
-    norm_rows(ONE)
+    start(g_pair(ONE, base))
+    norm_rows(n_ch - ONE)
     u_mid(NIL)
+    front_sent()
+    u_near(NIL)
+    for i in range(ONE, n_ch - ONE):
+        norm_rows(i)
     u_start(ONE)
-    front_sent()
-    for i in range(TWO, n_ch):
-        norm_rows(i)
-    u_last(NIL)
-    u_ready(NIL)
-
-    tasks = {"mid": u_mid, "last": u_last, "start": u_start, "e": t_e, "final": t_final, "fwd": t_fwd}
+    for j in range(THREE):
+        u_pair(NIL, j).wait_recv()
+
+    def gate_up(q, ranks):
+        return functools.reduce(jnp.add, [
+            jnp.dot(u2[rows_of(NIL, NIL, TWO * chunks[NIL]), cols(rank, col)], wbuf[(base + q) % slots, cols(rank, col)],
+                    preferred_element_type=F32) for rank in ranks])
+
+    def put_hidden(i, j, g, u):
+        g = (jax.nn.silu(g) * u).astype(BF16)
+        for q in range(FOUR):
+            hbuf[FOUR * j + q, top(TWO * chunks[i])] = g[:, q * LANES:(q + ONE) * LANES]
+
+    wait(g_pair(NIL, base))
+    r = chunks[NIL]
+
+    @pl.loop(NIL, TWO)
+    def _(q):
+        v = gate_up(q, (y, yp, ym))
+        for a in range(TWO):
+            for b in range(TWO):
+                d_in[ONE, FOUR * q + TWO * a + b, top(r)] = v[a * r:(a + ONE) * r, b * cb:(b + ONE) * cb]
+
+    u_far(NIL)
+    u_pair(NIL, THREE).wait_recv()
+    part_sums = [jnp.concatenate([jnp.concatenate([d_in[ONE, FOUR * q + TWO * a + b, top(r)] for b in range(TWO)], axis=ONE)
+                                  for a in range(TWO)], axis=NIL) for q in range(TWO)]
+    put_hidden(NIL, NIL, *[part_sums[q] + gate_up(q, (y2,)) for q in range(TWO)])
+
+    def t_own(i):
+        for q in range(FOUR):
+            t_add(i, FOUR * (n_d - ONE) + q)
+
+    tasks = {"own": t_own, "mid": u_mid, "last": u_last, "start": u_start, "e": t_e, "final": t_final, "fwd": t_fwd}
 
     def run(todo, at):
         for when, name, *args in todo:
@@ -635,7 +681,7 @@
         g_base, d_base = base % slots, (base + TWO * n_g) % slots
         base += TWO * (n_g + n_d)
 
-        @pl.loop(NIL, n_g)
+        @pl.loop(NIL if i else ONE, n_g)
         def _(j):
             @pl.when(j + ONE < n_g)
             def _():
@@ -646,11 +692,8 @@
                 start(d_pair(NIL, d_base))
 
             wait(g_pair(j, g_base))
-            g, u = (jnp.dot(u2[rows_of(i, NIL, TWO * r), :], wbuf[(g_base + TWO * j + q) % slots], preferred_element_type=F32)
-                    for q in range(TWO))
-            g = (jax.nn.silu(g) * u).astype(BF16)
-            for q in range(FOUR):
-                hbuf[FOUR * j + q, top(TWO * r)] = g[:, q * LANES:(q + ONE) * LANES]
+            put_hidden(i, j, *[jnp.dot(u2[rows_of(i, NIL, TWO * r), :], wbuf[(g_base + TWO * j + q) % slots],
+                                       preferred_element_type=F32) for q in range(TWO)])
             run(plan[i][NIL], j)
 
         if i:
@@ -674,6 +717,12 @@
             def _():
                 for q in range(FOUR):
                     d_copy(i, q, out + q).wait_send()
+
+            if i:
+                @pl.when(p < TWO)
+                def _():
+                    for q in range(FOUR):
+                        d_copy(i - ONE, q, out + q).wait_send()
 
             for q in range(TWO):
                 v = jnp.dot(wide_rows(NIL, TWO * r), wbuf[(d_base + TWO * p + q) % slots, top(ff)],
@@ -701,11 +750,11 @@
                     t_f(i, k)
             run(plan[i][ONE], p)
 
-        for q in range(FOUR):
-            t_add(i, FOUR * (n_d - ONE) + q)
-        for q in range(FOUR):
-            for out in range(TWO):
-                d_copy(i, q, FOUR * out + q).wait_send()
+        if i + ONE == n_ch:
+            for q in range(FOUR):
+                t_add(i, FOUR * (n_d - ONE) + q)
+            for q in range(EIGHT):
+                d_copy(i, q, q).wait_send()
         for name, *args in plan[i][TWO]:
             tasks[name](*args)
         if i + ONE < n_ch:
@@ -733,7 +782,7 @@
 def mlp_plan():
     early = lambda i: [(3, "e", i, 0, 1), (3, "e", i, 1, 1), (4, "e", i, 2, 1), (4, "e", i, 0, 0), (4, "e", i, 1, 0)]
     late = lambda i: [("e", i, 3, 1), ("e", i, 2, 0), ("e", i, 4, 1), ("e", i, 3, 0), ("e", i, 4, 0)]
-    at_start = lambda i: [(0, *t) for t in late(i)]
+    at_start = lambda i: [(0, *t) for t in late(i)] + [(0, "own", i)]
     finals = lambda i, at: [(a, "final", i, k) for k, a in enumerate(at)]
     passed = lambda i, at: [(a, "fwd", i, k) for k, a in enumerate(at)]
     gather = [(1, "mid", 1), (1, "start", 2), (3, "last", 1), (4, "mid", 2), (6, "last", 2)]
@@ -751,12 +800,13 @@
     nb = col // cb
     n_ch, rm = len(CHUNKS), max(CHUNKS)
     lanes = -(-rm // LANES) * LANES
-    rope_c, rope_s = rope_tables(positions)
+    half_dim = np.arange(HEAD_DIM) % (HEAD_DIM // TWO)
+    freq = jnp.asarray((ROPE_BASE ** (-half_dim * (2.0 / HEAD_DIM))).astype(np.float32)[None])
     dma = pltpu.SemaphoreType.DMA
     hbm, vmem = pl.BlockSpec(memory_space=pl.ANY), pl.BlockSpec(memory_space=pltpu.VMEM)
     bufs = [((FOUR, dim, TWO * cb), BF16), ((TWO * rows, dim), BF16), ((ff // LANES, rows, LANES), BF16),
-            ((heads, rows, HEAD_DIM), BF16), ((SUB, rows), F32), ((sp, SUB, rows), F32), ((rows, LANES), BF16),
-            ((sp, rows, LANES), BF16), ((col // LANES, rows, LANES), F32), ((n_ch, SUB, lanes), F32), ((n_ch, tp - ONE, SUB, lanes), F32),
+            ((heads, rows, HEAD_DIM), BF16), ((rows, HEAD_DIM), F32), ((rows, HEAD_DIM), F32), ((SUB, rows), F32), ((sp, SUB, rows), F32), ((rows, LANES), BF16),
+            ((col // LANES, rows, LANES), F32), ((n_ch, SUB, lanes), F32), ((n_ch, tp - ONE, SUB, lanes), F32),
             ((tp * nb * rm, cb), F32), ((EIGHT, rm, cb), F32), ((TWO, tp * nb, rm, cb), F32),
             ((TWO, TWO, nb, rm // TWO, cb), F32), ((TWO, TWO, nb, rm, cb), F32), ((TWO, nb, rm, cb), BF16)]
     sems = [(FOUR,), (FOUR, TWO), (sp,), (sp,)] + [(n_kv, TWO)] * FOUR + [(n_kv, FOUR)] * TWO + [(tp - ONE,)] * TWO
@@ -772,9 +822,37 @@
         in_specs=[hbm] + [vmem] * (FOUR + ONE) + [hbm] * (FOUR + THREE), out_specs=[hbm] * (FOUR + ONE),
         scratch_shapes=[pltpu.VMEM(*b) for b in bufs] + [dma(q) for q in sems],
         compiler_params=pltpu.CompilerParams(collective_id=ONE, has_side_effects=True, vmem_limit_bytes=VMEM_BYTES),
-    )(x_in, segments.reshape(ONE, rows), rope_c, rope_s, gain_a.reshape(ONE, dim), gain_m.reshape(ONE, dim),
+    )(x_in, segments.reshape(ONE, rows), positions.reshape(ONE, rows), freq, gain_a.reshape(ONE, dim), gain_m.reshape(ONE, dim),
       wq, wk, wv, wo, wg, wu, wd)
-    return y_out, kc, vc
+    return copy_out(y_out, kc, vc)
+
+
+def copy_kernel(*refs):
+    n = len(refs) // FOUR
+    ins, outs, bufs, sems = (refs[i * n:(i + ONE) * n] for i in range(FOUR))
+
+    def parts(src, dst, sem):
+        step = src.shape[NIL] // sem.shape[ONE]
+        return [(src.at[pl.ds(k * step, step)], dst.at[pl.ds(k * step, step)], k) for k in range(sem.shape[ONE])]
+
+    for a, b, sem in zip(ins, bufs, sems):
+        start([pltpu.make_async_copy(x, v, sem.at[NIL, k]) for x, v, k in parts(a, b, sem)])
+    for a, b, o, sem in zip(ins, bufs, outs, sems):
+        for (x, v, k), (_, d, _) in zip(parts(a, b, sem), parts(b, o, sem)):
+            pltpu.make_async_copy(x, v, sem.at[NIL, k]).wait()
+            pltpu.make_async_copy(v, d, sem.at[ONE, k]).start()
+    for b, o, sem in zip(bufs, outs, sems):
+        wait([pltpu.make_async_copy(v, d, sem.at[ONE, k]) for v, d, k in parts(b, o, sem)])
+
+
+def copy_out(*arrays):
+    hbm = pl.BlockSpec(memory_space=pl.ANY)
+    return pl.pallas_call(
+        copy_kernel, name="copy_out", out_shape=[jax.ShapeDtypeStruct(a.shape, a.dtype) for a in arrays],
+        in_specs=[hbm] * len(arrays), out_specs=[hbm] * len(arrays),
+        scratch_shapes=[pltpu.VMEM(a.shape, a.dtype) for a in arrays] + [pltpu.SemaphoreType.DMA((TWO, FOUR)) for _ in arrays],
+        compiler_params=pltpu.CompilerParams(vmem_limit_bytes=VMEM_BYTES),
+    )(*arrays)
 
 
 def solution(mesh):

time: 305 us -> 290 us (0.951)
  the two profiles are of different devices: /device:TPU:102 before, /device:TPU:97 now
where the time goes in v4:
time: 290 us; the launch traced here: 288 us
  Pallas kernels  287 us (99%)
    pallas_call x1, Pallas kernels, layer_call(): pl.pallas_call(functools.partial(layer_kernel, CHUNKS, cb, mlp_plan()), n...  281 us
    pallas_call x1, Pallas kernels, copy_out(): pl.pallas_call(copy_kernel, name='copy_out', out_shape=[jax.ShapeDtypeStr...  6.17 us

profile of v4, /device:TPU:97, one launch (start us, length us, event | category | flops | bytes accessed | tf_op | source)
XLA Modules:
  0.0 288.2 jit_solution(12551602130834580325)
XLA Ops:
  0.6 281.2 %layer.1 = (bf16[4096,128]{1,0:T(8,128)(2,1)}, bf16[4096,128]{1,0:T(8,128)(2,1)}, bf16[512,4096]{1,0:T(8,128)(2,1)}, bf16[3,1024,1280]{2,1,0:T(8,128)(2,1)}, bf16[512,5120]{1,0:T(8,128)(2,1)}) custom-call(bf16[512,5120]{1,0:T(8,128)(2,1)} %x_hbm.1, s32[1,512]{1,0:T(1,128)} %bitcast.8, s32[1,512]{1,0:T(1,128)} %bitcast.9, f32[1,128]{1,0:T(1,128)} %constant.2.clone.freq, ...), custom_call_target="tpu_custom_call" | custom-call | tf_op jit(solution)/shard_map/layer/pallas_call | solution.py:818
  281.9 6.2 %copy_out.1 = (bf16[512,5120]{1,0:T(8,128)(2,1)}, bf16[4096,128]{1,0:T(8,128)(2,1)}, bf16[4096,128]{1,0:T(8,128)(2,1)}) custom-call(bf16[512,5120]{1,0:T(8,128)(2,1)} %get-tuple-element.9.refs_0_, bf16[4096,128]{1,0:T(8,128)(2,1)} %get-tuple-element.10.refs_1_, bf16[4096,128]{1,0:T(8,128)(2,1)} %get-tuple-element.11.refs_2_), custom_call_target="tpu_custom_call" | custom-call | tf_op jit(solution)/shard_map/copy_out/pallas_call | solution.py:850

commit v5 on v4

--- a/solution.py
+++ b/solution.py
@@ -2,7 +2,6 @@
 
 import jax
 import jax.numpy as jnp
-import numpy as np
 from jax import lax
 from jax.experimental import pallas as pl
 from jax.experimental.pallas import tpu as pltpu
@@ -40,10 +39,10 @@
 
 
 def layer_kernel(chunks, cb, plan, x_hbm, seg, pos, freq, gain_a, gain_m, wq, wk, wv, wo, wg, wu, wd,
-                 kc, vc, attn, wo_g, y_hbm,
+                 kc, vc, wo_g, y_hbm,
                  wbuf, u2, hbuf, qb, rope_c, rope_s, seg_row, sgb, fq, xmid, srow, sin, p_own, p_out, d_in, f_in, e_in, ystage,
                  xsem, wsem, sg_s, sg_r, k1s, k1r, k2s, k2r, kps, kpr, w1s, w1r, w2s, w2r, w3s, w3r, wps, wpr,
-                 t_s, t_r, v_s, v_r, csem, lsem, osem, xrsem,
+                 t_s, t_r, v_s, v_r, csem, osem, xrsem,
                  s_s, s_r, u1s, u1r, u2s, u2r, ups, upr, d_s, d_r, f_s, f_r, e_s, e_r, a_l, a_s, a_r, h_s, h_r):
     rows, dim = x_hbm.shape
     tp, sp = lax.axis_size("tp"), lax.axis_size("sp")
@@ -126,15 +125,15 @@
 
     def w2(i, side):
         b = w_blk(i, s, NIL, wrow)
-        return remote(b, b, w2s.at[i, side], w2r.at[i, ONE - side], (to_up, to_dn)[side])
+        return remote(b, b, w2s.at[side], w2r.at[i, ONE - side], (to_up, to_dn)[side])
 
     def w3(i, side):
         b = w_blk(i, (up, dn)[side], (half, NIL)[side], half)
-        return remote(b, b, w3s.at[i, side], w3r.at[i, side], (to_dn, to_up)[side])
+        return remote(b, b, w3s.at[side], w3r.at[i, side], (to_dn, to_up)[side])
 
     def wp(i, j):
         b = w_blk(i, (s, up, dn, far)[j], NIL, wrow)
-        return remote(b, b, wps.at[i, j], wpr.at[i, j], to_pair)
+        return remote(b, b, wps.at[j], wpr.at[i, j], to_pair)
 
     def w_start(i):
         w1(tp - ONE - i).wait_recv()
@@ -285,14 +284,15 @@
             xmid[i] = xmid[i] * al + o
 
     def a_at(rank, h, r0, n):
-        return attn.at[pl.ds(r0, n), aligned(rank * wide + h * hd, hd)]
+        b = rank * heads + h
+        return wbuf.at[slots - ONE, pl.ds(pl.multiple_of(b // FOUR * rows + r0, LANES), n), aligned(b % FOUR * hd, hd)]
 
     def a1(h, side):
-        return remote(qb.at[h], a_at(y, h, NIL, rows), t_s.at[side, h], t_r.at[ONE - side, h], (to_p, to_m)[side])
+        return remote(qb.at[h], a_at(y, h, NIL, rows), t_s.at[side], t_r.at[ONE - side, h], (to_p, to_m)[side])
 
     def a2(h, side):
         b = a_at((yp, ym)[side], h, (rows // TWO, NIL)[side], rows // TWO)
-        return remote(b, b, v_s.at[side, h], v_r.at[side, h], (to_m, to_p)[side])
+        return remote(b, b, v_s.at[side], v_r.at[side], (to_m, to_p)[side])
 
     def pass_on(h):
         for side in range(TWO):
@@ -308,8 +308,7 @@
 
         kp(g, NIL).wait_recv()
 
-        @pl.loop(NIL, group)
-        def _(i):
+        def own_keys(i):
             @pl.when(core == NIL)
             def _():
                 attend(g * group + i, i, g, s, ONE, True)
@@ -317,6 +316,11 @@
             @pl.when(core == ONE)
             def _():
                 attend(g * group + i, i, g, chip_at(NIL), TWO, True)
+
+        @pl.when(g == NIL)
+        def _():
+            pl.loop(NIL, group)(own_keys)
+            w_start(NIL)
 
         k_last(g)
         for j in range(ONE, FOUR):
@@ -325,6 +329,10 @@
         @pl.loop(NIL, group)
         def _(i):
             h = g * group + i
+
+            @pl.when(g > NIL)
+            def _():
+                own_keys(i)
 
             @pl.loop(ONE, n_chip)
             def _(e):
@@ -340,7 +348,7 @@
             @pl.when(h == NIL)
             def _():
                 k_mid(ONE)
-                for b in range(tp - ONE):
+                for b in range(ONE, tp - ONE):
                     w_start(b)
 
             for b in range(tp - TWO):
@@ -356,9 +364,8 @@
     caches = [pltpu.make_async_copy(hbuf.at[d * per_dev + TWO * mine_kv + i], c.at[pl.ds(d * rows, rows)], csem.at[i, d])
               for i, c in enumerate((kc, vc)) for d in range(sp)]
     start(caches)
+    w_mid(tp - TWO)
     pass_on(heads - TWO)
-    w_mid(tp - TWO)
-    pass_on(heads - ONE)
 
     def w_done(i):
         for j in range(FOUR):
@@ -366,52 +373,47 @@
         for t in range(n_o):
             o_part(t, i + ONE).start()
 
-    for g in range(n_kv):
-        for j in range(FOUR):
-            kp(g, j).wait_send()
-        for side in range(TWO):
-            k1(g, side).wait_send()
-            k2(g, side).wait_send()
-    wait(caches)
-
-    def head_in(d, h):
-        rank = (y + d) % tp
-        return pltpu.make_async_copy(a_at(rank, h, NIL, rows), hbuf.at[rank * heads + h], lsem.at[d, h])
-
+    for i in range(tp - ONE):
+        if i == tp - TWO:
+            pass_on(heads - ONE)
+        w_last(i)
+    for i in range(tp - TWO):
+        w_done(i)
     for h in range(heads):
-        hbuf[y * heads + h] = qb[h]
-        head_in(ONE, h).start()
-        head_in(THREE, h).start()
-
-    for i in range(tp - ONE):
-        w_last(i)
-        if i:
-            w_done(i - ONE)
-    for h in range(heads):
-        for side in range(TWO):
-            a2(h, side).wait_recv()
-        head_in(TWO, h).start()
+        b = y * heads + h
+        wbuf[slots - ONE, aligned(b // FOUR * rows, rows), aligned(b % FOUR * hd, hd)] = qb[h]
+
+    def all_heads(side, n, send, recv):
+        b = qb.at[:, top(n)]
+        return remote(b, b, send.at[side], recv.at[side], to_p)
+
+    for side in range(TWO):
+        all_heads(side, rows // TWO, v_s, v_r).wait_recv()
+        all_heads(side, rows // TWO, v_s, v_r).wait_send()
     w_done(tp - TWO)
-    for h in range(heads):
-        for d in range(ONE, tp):
-            head_in(d, h).wait()
-
-    def wide_rows(r0, n):
-        return jnp.concatenate([hbuf[b, pl.ds(r0, n)] for b in range(hbuf.shape[NIL])], axis=ONE)
+
+    def attn_rows(r0, n):
+        return jnp.concatenate([wbuf[slots - ONE, pl.ds(b * rows + r0, n), :] for b in range(tp * heads // FOUR)], axis=ONE)
+
+    def wide_rows(n):
+        return jnp.concatenate([hbuf[b, top(n)] for b in range(hbuf.shape[NIL])], axis=ONE)
 
     def front_sent():
-        @pl.loop(NIL, heads)
-        def _(h):
+        for g in range(n_kv):
+            for j in range(FOUR):
+                kp(g, j).wait_send()
             for side in range(TWO):
-                a1(h, side).wait_send()
-                a2(h, side).wait_send()
+                k1(g, side).wait_send()
+                k2(g, side).wait_send()
+        wait(caches)
+        for side in range(TWO):
+            all_heads(side, rows, t_s, v_r).wait_send()
+        for n, send, recv in ((wrow, wps, wpr), (wrow, w2s, w2r), (half, w3s, w3r)):
+            b = wo_g.at[:, top(n)]
+            for j in range(send.shape[NIL]):
+                remote(b, b, send.at[j], recv.at[NIL, NIL], to_p).wait_send()
         for i in range(tp - ONE):
             w1(i + ONE).wait_send()
-            for j in range(FOUR):
-                wp(i, j).wait_send()
-            for side in range(TWO):
-                w2(i, side).wait_send()
-                w3(i, side).wait_send()
         for j in range(ONE, sp):
             sg(j).wait_send()
 
@@ -446,7 +448,7 @@
     def x1_rows(i):
         r0, r = starts[i], chunks[i]
         def tile(t, w):
-            v = jnp.dot(wide_rows(r0, r), wbuf[t, top(tp * part), top(w)], preferred_element_type=F32)
+            v = jnp.dot(attn_rows(r0, r), wbuf[t, top(tp * part), top(w)], preferred_element_type=F32)
             for q in range(w // LANES):
                 xmid[t * FOUR + q, pl.ds(r0, r)] = v[:, q * LANES:(q + ONE) * LANES]
 
@@ -542,19 +544,20 @@
     def blk_rows(m, row0, n):
         return pl.ds(pl.multiple_of(m * max(chunks) + row0, EIGHT), n)
 
-    def d_copy(i, m, slot):
+    def d_copy(i, p, out):
         r, par = chunks[i], i % TWO
-        return remote(p_out.at[slot, top(r)], d_in.at[par, m, top(r)], d_s.at[slot], d_r.at[par, m], to_pair)
-
-    def t_add(i, m):
+        return remote(p_out.at[out, :, top(r)], d_in.at[par, pl.ds(FOUR * p, FOUR), top(r)], d_s.at[out], d_r.at[par, p], to_pair)
+
+    def t_add(i, p):
         r, par = chunks[i], i % TWO
-        d_copy(i, m, NIL).wait_recv()
-        p_own[blk_rows(m, NIL, r), :] += d_in[par, m, top(r)]
+        d_copy(i, p, NIL).wait_recv()
+        for q in range(FOUR):
+            p_own[blk_rows(FOUR * p + q, NIL, r), :] += d_in[par, FOUR * p + q, top(r)]
 
     def f_copy(i, k, side):
         h, par = chunks[i] // TWO, i % TWO
         return remote(p_own.at[blk_rows(k, side * h, h)], f_in.at[par, side, k, top(h)],
-                      f_s.at[side, k], f_r.at[par, side, k], (to_m, to_p)[side])
+                      f_s.at[side], f_r.at[par, side, k], (to_m, to_p)[side])
 
     def t_f(i, k):
         f_copy(i, k, NIL).start()
@@ -563,7 +566,7 @@
     def e_copy(i, k, side):
         r, par = chunks[i], i % TWO
         return remote(p_own.at[blk_rows((TWO - side) * nb + k, NIL, r)], e_in.at[par, side, k, top(r)],
-                      e_s.at[side, k], e_r.at[par, side, k], (to_m, to_p)[side])
+                      e_s.at[side], e_r.at[par, side, k], (to_m, to_p)[side])
 
     def t_e(i, k, side):
         h, par = chunks[i] // TWO, i % TWO
@@ -576,17 +579,17 @@
 
     def a_copy_y(i, k, side):
         r, par = chunks[i], i % TWO
-        return remote(ystage.at[par, k, top(r)], y_at(i, NIL, r, y, k), a_s.at[par, side, k], a_r.at[par, ONE - side, k],
+        return remote(ystage.at[par, k, top(r)], y_at(i, NIL, r, y, k), a_s.at[par, side], a_r.at[par, ONE - side, k],
                       (to_p, to_m)[side])
 
     def a_local(i, k):
         r, par = chunks[i], i % TWO
-        return pltpu.make_async_copy(ystage.at[par, k, top(r)], y_at(i, NIL, r, y, k), a_l.at[par, k])
+        return pltpu.make_async_copy(ystage.at[par, k, top(r)], y_at(i, NIL, r, y, k), a_l.at[par])
 
     def h_copy(i, k, side):
         h = chunks[i] // TWO
         b = y_at(i, h, h, yp, k) if side == NIL else y_at(i, NIL, h, ym, k)
-        return remote(b, b, h_s.at[i, side, k], h_r.at[i, side, k], (to_m, to_p)[side])
+        return remote(b, b, h_s.at[i, side], h_r.at[i, side], (to_m, to_p)[side])
 
     def t_final(i, k):
         r, par = chunks[i], i % TWO
@@ -605,20 +608,20 @@
             h_copy(i, k, side).start()
 
     def sums_sent(i):
-        for k in range(nb):
-            for side in range(TWO):
-                f_copy(i, k, side).wait_send()
-                e_copy(i, k, side).wait_send()
+        for side in range(TWO):
+            for n, send, recv in ((chunks[i] // TWO, f_s, f_r), (chunks[i], e_s, e_r)):
+                b = p_own.at[top(nb * n)]
+                remote(b, b, send.at[side], recv.at[NIL, NIL, NIL], to_p).wait_send()
 
     def rows_done(i):
-        for k in range(nb):
-            for side in range(TWO):
-                h_copy(i, k, side).wait_recv()
-                h_copy(i, k, side).wait_send()
-                a_copy_y(i, k, side).wait_send()
-            a_local(i, k).wait()
-
-    g_tile(NIL, base, NIL).start()
+        r, par = chunks[i], i % TWO
+        b = y_hbm.at[pl.ds(starts[i], r), cols(y, col)]
+        pltpu.make_async_copy(b, b, a_l.at[par]).wait()
+        for side in range(TWO):
+            remote(b, b, a_s.at[par, side], a_r.at[par, side, NIL], to_p).wait_send()
+            c = y_hbm.at[pl.ds(starts[i], r // TWO), cols(y, col)]
+            remote(c, c, h_s.at[i, side], h_r.at[i, side], to_p).wait()
+
     wait(xr_copies)
     x1_rows(NIL)
     x1_rows(n_ch - ONE)
@@ -626,15 +629,12 @@
     u_start(NIL)
     for i in range(ONE, n_ch - ONE):
         x1_rows(i)
-    g_tile(NIL, NIL, ONE).start()
+    start(g_pair(NIL, base))
     start(g_pair(ONE, base))
     norm_rows(n_ch - ONE)
     u_mid(NIL)
     front_sent()
     u_near(NIL)
-    for i in range(ONE, n_ch - ONE):
-        norm_rows(i)
-    u_start(ONE)
     for j in range(THREE):
         u_pair(NIL, j).wait_recv()
 
@@ -659,14 +659,16 @@
                 d_in[ONE, FOUR * q + TWO * a + b, top(r)] = v[a * r:(a + ONE) * r, b * cb:(b + ONE) * cb]
 
     u_far(NIL)
+    for i in range(ONE, n_ch - ONE):
+        norm_rows(i)
+    u_start(ONE)
     u_pair(NIL, THREE).wait_recv()
     part_sums = [jnp.concatenate([jnp.concatenate([d_in[ONE, FOUR * q + TWO * a + b, top(r)] for b in range(TWO)], axis=ONE)
                                   for a in range(TWO)], axis=NIL) for q in range(TWO)]
     put_hidden(NIL, NIL, *[part_sums[q] + gate_up(q, (y2,)) for q in range(TWO)])
 
     def t_own(i):
-        for q in range(FOUR):
-            t_add(i, FOUR * (n_d - ONE) + q)
+        t_add(i, n_d - ONE)
 
     tasks = {"own": t_own, "mid": u_mid, "last": u_last, "start": u_start, "e": t_e, "final": t_final, "fwd": t_fwd}
 
@@ -711,33 +713,29 @@
                     start(g_pair(NIL, base % slots))
 
             wait(d_pair(p, d_base))
-            out = p % TWO * FOUR
+            out = p % TWO
 
             @pl.when(p >= TWO)
             def _():
-                for q in range(FOUR):
-                    d_copy(i, q, out + q).wait_send()
+                d_copy(i, NIL, out).wait_send()
 
             if i:
                 @pl.when(p < TWO)
                 def _():
-                    for q in range(FOUR):
-                        d_copy(i - ONE, q, out + q).wait_send()
+                    d_copy(i - ONE, NIL, out).wait_send()
 
             for q in range(TWO):
-                v = jnp.dot(wide_rows(NIL, TWO * r), wbuf[(d_base + TWO * p + q) % slots, top(ff)],
+                v = jnp.dot(wide_rows(TWO * r), wbuf[(d_base + TWO * p + q) % slots, top(ff)],
                             preferred_element_type=F32)
                 for e in range(TWO):
                     b = TWO * q + e
                     p_own[blk_rows(FOUR * p + b, NIL, r), :] = v[:r, e * cb:(e + ONE) * cb]
-                    p_out[out + b, top(r)] = v[r:, e * cb:(e + ONE) * cb]
-            for q in range(FOUR):
-                d_copy(i, FOUR * p + q, out + q).start()
+                    p_out[out, b, top(r)] = v[r:, e * cb:(e + ONE) * cb]
+            d_copy(i, p, out).start()
 
             @pl.when(p >= ONE)
             def _():
-                for q in range(FOUR):
-                    t_add(i, FOUR * (p - ONE) + q)
+                t_add(i, p - ONE)
 
             @pl.when(p == ONE)
             def _():
@@ -751,10 +749,9 @@
             run(plan[i][ONE], p)
 
         if i + ONE == n_ch:
-            for q in range(FOUR):
-                t_add(i, FOUR * (n_d - ONE) + q)
-            for q in range(EIGHT):
-                d_copy(i, q, q).wait_send()
+            t_add(i, n_d - ONE)
+            for out in range(TWO):
+                d_copy(i, NIL, out).wait_send()
         for name, *args in plan[i][TWO]:
             tasks[name](*args)
         if i + ONE < n_ch:
@@ -785,7 +782,7 @@
     at_start = lambda i: [(0, *t) for t in late(i)] + [(0, "own", i)]
     finals = lambda i, at: [(a, "final", i, k) for k, a in enumerate(at)]
     passed = lambda i, at: [(a, "fwd", i, k) for k, a in enumerate(at)]
-    gather = [(1, "mid", 1), (1, "start", 2), (3, "last", 1), (4, "mid", 2), (6, "last", 2)]
+    gather = [(2, "mid", 1), (2, "start", 2), (4, "last", 1), (5, "mid", 2), (7, "last", 2)]
     return ((gather, early(0), ()),
             (at_start(0) + finals(0, (1, 2, 3, 4, 5)) + passed(0, (5, 6, 6, 6, 7)), early(1), ()),
             (at_start(1) + finals(1, (2, 3, 4, 6, 7)), passed(1, (0, 1, 1, 2, 2)) + early(2), late(2)))
@@ -800,26 +797,27 @@
     nb = col // cb
     n_ch, rm = len(CHUNKS), max(CHUNKS)
     lanes = -(-rm // LANES) * LANES
-    half_dim = np.arange(HEAD_DIM) % (HEAD_DIM // TWO)
-    freq = jnp.asarray((ROPE_BASE ** (-half_dim * (2.0 / HEAD_DIM))).astype(np.float32)[None])
+    half_dim = (jnp.arange(HEAD_DIM) % (HEAD_DIM // TWO)).astype(F32)
+    freq = jnp.power(F32(ROPE_BASE), -half_dim * (2.0 / HEAD_DIM))[None]
     dma = pltpu.SemaphoreType.DMA
     hbm, vmem = pl.BlockSpec(memory_space=pl.ANY), pl.BlockSpec(memory_space=pltpu.VMEM)
     bufs = [((FOUR, dim, TWO * cb), BF16), ((TWO * rows, dim), BF16), ((ff // LANES, rows, LANES), BF16),
             ((heads, rows, HEAD_DIM), BF16), ((rows, HEAD_DIM), F32), ((rows, HEAD_DIM), F32), ((SUB, rows), F32), ((sp, SUB, rows), F32), ((rows, LANES), BF16),
             ((col // LANES, rows, LANES), F32), ((n_ch, SUB, lanes), F32), ((n_ch, tp - ONE, SUB, lanes), F32),
-            ((tp * nb * rm, cb), F32), ((EIGHT, rm, cb), F32), ((TWO, tp * nb, rm, cb), F32),
+            ((tp * nb * rm, cb), F32), ((TWO, FOUR, rm, cb), F32), ((TWO, tp * nb, rm, cb), F32),
             ((TWO, TWO, nb, rm // TWO, cb), F32), ((TWO, TWO, nb, rm, cb), F32), ((TWO, nb, rm, cb), BF16)]
     sems = [(FOUR,), (FOUR, TWO), (sp,), (sp,)] + [(n_kv, TWO)] * FOUR + [(n_kv, FOUR)] * TWO + [(tp - ONE,)] * TWO
-    sems += [(tp - ONE, TWO)] * FOUR + [(tp - ONE, FOUR)] * TWO + [(TWO, heads)] * FOUR + [(TWO, sp), (tp, heads), (THREE, tp), (n_ch,)]
+    sems += [(TWO,), (tp - ONE, TWO)] * TWO + [(FOUR,), (tp - ONE, FOUR)] + [(TWO,), (TWO, heads), (TWO,), (TWO,)]
+    sems += [(TWO, sp), (THREE, tp), (n_ch,)]
     sems += [(n_ch, tp - ONE)] * TWO + [(n_ch, TWO, TWO)] * TWO + [(n_ch, TWO)] * TWO + [(n_ch, FOUR)] * TWO
-    sems += [(EIGHT,), (TWO, tp * nb)] + [(TWO, nb), (TWO, TWO, nb)] * TWO + [(TWO, nb)] + [(TWO, TWO, nb)] * TWO
-    sems += [(n_ch, TWO, nb)] * TWO
+    sems += [(TWO,), (TWO, tp * nb // FOUR)] + [(TWO,), (TWO, TWO, nb)] * TWO + [(TWO,), (TWO, TWO), (TWO, TWO, nb)]
+    sems += [(n_ch, TWO)] * TWO
     cache = jax.ShapeDtypeStruct((sp * rows, HEAD_DIM), BF16)
-    kc, vc, _, _, y_out = pl.pallas_call(
+    kc, vc, _, y_out = pl.pallas_call(
         functools.partial(layer_kernel, CHUNKS, cb, mlp_plan()), name="layer",
-        out_shape=[cache, cache, jax.ShapeDtypeStruct((rows, tp * heads * HEAD_DIM), BF16), jax.ShapeDtypeStruct((tp - ONE, wo.shape[NIL], col), BF16),
+        out_shape=[cache, cache, jax.ShapeDtypeStruct((tp - ONE, wo.shape[NIL], col), BF16),
                    jax.ShapeDtypeStruct((rows, dim), BF16)],
-        in_specs=[hbm] + [vmem] * (FOUR + ONE) + [hbm] * (FOUR + THREE), out_specs=[hbm] * (FOUR + ONE),
+        in_specs=[hbm] + [vmem] * (FOUR + ONE) + [hbm] * (FOUR + THREE), out_specs=[hbm] * FOUR,
         scratch_shapes=[pltpu.VMEM(*b) for b in bufs] + [dma(q) for q in sems],
         compiler_params=pltpu.CompilerParams(collective_id=ONE, has_side_effects=True, vmem_limit_bytes=VMEM_BYTES),
     )(x_in, segments.reshape(ONE, rows), positions.reshape(ONE, rows), freq, gain_a.reshape(ONE, dim), gain_m.reshape(ONE, dim),

time: 290 us -> 285 us (0.983)
  Pallas kernels: 287 us -> 282 us
    pallas_call x1, Pallas kernels: 281 us -> 275 us  [layer_call(): pl.pallas_call(functools.partial(layer_kernel, CHUNKS, cb, mlp_plan()), n...]
where the time goes in v5:
time: 285 us; the launch traced here: 283 us
  Pallas kernels  282 us (99%)
    pallas_call x1, Pallas kernels, layer_call(): pl.pallas_call(functools.partial(layer_kernel, CHUNKS, cb, mlp_plan()), n...  275 us
    pallas_call x1, Pallas kernels, copy_out(): pl.pallas_call(copy_kernel, name='copy_out', out_shape=[jax.ShapeDtypeStr...  6.17 us

profile of v5, /device:TPU:97, one launch (start us, length us, event | category | flops | bytes accessed | tf_op | source)
XLA Modules:
  0.0 282.9 jit_solution(14527396897321176223)
XLA Ops:
  0.6 0.5 fusion.3.freq
  1.2 275.4 %layer.1 = (bf16[4096,128]{1,0:T(8,128)(2,1)}, bf16[4096,128]{1,0:T(8,128)(2,1)}, bf16[3,1024,1280]{2,1,0:T(8,128)(2,1)}, bf16[512,5120]{1,0:T(8,128)(2,1)}) custom-call(bf16[512,5120]{1,0:T(8,128)(2,1)} %x_hbm.1, s32[1,512]{1,0:T(1,128)} %bitcast.8, s32[1,512]{1,0:T(1,128)} %bitcast.9, f32[1,128]{1,0:T(1,128)} %fusion.3.freq, f32[1,5120]{1,0:T(1,128)} %bitcast.6, ...), custom_call_target="tpu_custom_call" | custom-call | tf_op jit(solution)/shard_map/layer/pallas_call | solution.py:816
  276.6 6.2 %copy_out.1 = (bf16[512,5120]{1,0:T(8,128)(2,1)}, bf16[4096,128]{1,0:T(8,128)(2,1)}, bf16[4096,128]{1,0:T(8,128)(2,1)}) custom-call(bf16[512,5120]{1,0:T(8,128)(2,1)} %get-tuple-element.9.refs_0_, bf16[4096,128]{1,0:T(8,128)(2,1)} %get-tuple-element.10.refs_1_, bf16[4096,128]{1,0:T(8,128)(2,1)} %get-tuple-element.11.refs_2_), custom_call_target="tpu_custom_call" | custom-call | tf_op jit(solution)/shard_map/copy_out/pallas_call | solution.py:848

commit v6 on v5

--- a/solution.py
+++ b/solution.py
@@ -784,8 +784,8 @@
     passed = lambda i, at: [(a, "fwd", i, k) for k, a in enumerate(at)]
     gather = [(2, "mid", 1), (2, "start", 2), (4, "last", 1), (5, "mid", 2), (7, "last", 2)]
     return ((gather, early(0), ()),
-            (at_start(0) + finals(0, (1, 2, 3, 4, 5)) + passed(0, (5, 6, 6, 6, 7)), early(1), ()),
-            (at_start(1) + finals(1, (2, 3, 4, 6, 7)), passed(1, (0, 1, 1, 2, 2)) + early(2), late(2)))
+            (at_start(0) + finals(0, (1, 2, 3, 4, 5)) + passed(0, (6, 6, 7, 7, 7)), early(1), ()),
+            (at_start(1) + finals(1, (2, 3, 4, 5, 6)), passed(1, (0, 0, 0, 1, 1)) + early(2), late(2)))
 
 
 def layer_call(x_in, positions, segments, gain_a, gain_m, wq, wk, wv, wo, wg, wu, wd):

time: 285 us -> 282 us (0.989)
  Pallas kernels: 282 us -> 279 us
    pallas_call x1, Pallas kernels: 275 us -> 272 us  [layer_call(): pl.pallas_call(functools.partial(layer_kernel, CHUNKS, cb, mlp_plan()), n...]
where the time goes in v6:
time: 282 us; the launch traced here: 280 us
  Pallas kernels  279 us (99%)
    pallas_call x1, Pallas kernels, layer_call(): pl.pallas_call(functools.partial(layer_kernel, CHUNKS, cb, mlp_plan()), n...  272 us
    pallas_call x1, Pallas kernels, copy_out(): pl.pallas_call(copy_kernel, name='copy_out', out_shape=[jax.ShapeDtypeStr...  6.17 us

profile of v6, /device:TPU:97, one launch (start us, length us, event | category | flops | bytes accessed | tf_op | source)
XLA Modules:
  0.0 279.9 jit_solution(16960859631109223038)
XLA Ops:
  0.6 0.5 fusion.3.freq
  1.2 272.4 %layer.1 = (bf16[4096,128]{1,0:T(8,128)(2,1)}, bf16[4096,128]{1,0:T(8,128)(2,1)}, bf16[3,1024,1280]{2,1,0:T(8,128)(2,1)}, bf16[512,5120]{1,0:T(8,128)(2,1)}) custom-call(bf16[512,5120]{1,0:T(8,128)(2,1)} %x_hbm.1, s32[1,512]{1,0:T(1,128)} %bitcast.8, s32[1,512]{1,0:T(1,128)} %bitcast.9, f32[1,128]{1,0:T(1,128)} %fusion.3.freq, f32[1,5120]{1,0:T(1,128)} %bitcast.6, ...), custom_call_target="tpu_custom_call" | custom-call | tf_op jit(solution)/shard_map/layer/pallas_call | solution.py:816
  273.5 6.2 %copy_out.1 = (bf16[512,5120]{1,0:T(8,128)(2,1)}, bf16[4096,128]{1,0:T(8,128)(2,1)}, bf16[4096,128]{1,0:T(8,128)(2,1)}) custom-call(bf16[512,5120]{1,0:T(8,128)(2,1)} %get-tuple-element.9.refs_0_, bf16[4096,128]{1,0:T(8,128)(2,1)} %get-tuple-element.10.refs_1_, bf16[4096,128]{1,0:T(8,128)(2,1)} %get-tuple-element.11.refs_2_), custom_call_target="tpu_custom_call" | custom-call | tf_op jit(solution)/shard_map/copy_out/pallas_call | solution.py:848
